TPU v7x, 32 devices: a whole 2x2x4 slice. The times are simulated.
32 devices in a mesh: groups: 2 (over y), ep: 8 (over z, core), tp: 2 (over x).
Axes of the slice: x: 2, y: 2, z: 4, core: 2. Of those that a mesh axis runs over, the one named last changes fastest.
Arguments:
- hidden: bfloat16 [1024, 2880], P(('groups', 'ep')), parts along dimension 0, may hold values from -6 to 6
- route_experts: int32 [1024, 4], P(('groups', 'ep')), parts along dimension 0, may hold values from 0 to 7, all different within a row; in each aligned block of 64 rows (0 to 63, 64 to 127, ...) at most 64 rows name the same one
- route_weight: float32 [1024, 4], P(('groups', 'ep')), parts along dimension 0, may hold values from 0.1 to 0.6
- norm_gain: bfloat16 [2880], replicated, may hold values from 0.099609375 to 1.8984375
- gate_up_codes: int32 [8, 360, 5120], P('ep', None, 'tp'), may hold values from -2147483648 to 2147483646
- gate_up_scales: bfloat16 [8, 90, 5120], P('ep', None, 'tp'), as said below
- gate_up_bias: bfloat16 [8, 5120], P('ep', 'tp'), may hold values from -3 to 3
- down_codes: int32 [8, 2560, 360], P('ep', 'tp'), may hold values from -2147483648 to 2147483646
- down_scales: bfloat16 [8, 80, 2880], P('ep', 'tp'), as said below
- down_bias: bfloat16 [8, 2880], P('ep', 'tp'), may hold values from -3 to 3
Outputs:
- layer_out: bfloat16 [1024, 2880], P(('groups', 'ep'), 'tp'), parts along dimension 0
There are 2 independent parts, one for each index of `groups`. A program takes and returns all parts, laid end to end along the dimension named above; an argument that names none is the same for every part. Nothing has to cross between parts.
Inputs may be any that keep to these rules, and one draw needn't show every extreme that they name: `route_experts`: each row names 4 different experts. In each aligned block of 64 rows no expert is named by more than 64 rows, and in some blocks one expert is named by exactly 64 rows. `gate_up_scales`: every scale is a power of two. `down_scales`: every scale is a power of two.
All inputs are finite; a program needn't handle non-finite values.
Results may differ from a plain program's by a relative error of at most 0.013.
Values may be sent and summed in bfloat16 or wider, within the bound.
A program may use at most 128 MiB of HBM per device.

v0:
```python
import functools

import jax
import jax.numpy as jnp
from jax import lax
from jax.experimental import pallas as pl
from jax.experimental.pallas import tpu as pltpu
from jax.sharding import PartitionSpec as P

MAGNITUDES = 0xC8643210 - (1 << 32)
SPARE = 64


def decode_nibble(nibble):
    magnit = nibble & 7
    exponent = jnp.maximum(jnp.right_shift(magnit, 1) - 1, 0)
    doubled = jnp.where(magnit < 2, magnit, jnp.left_shift(2 + (magnit & 1), exponent))
    signed_val = doubled.astype(jnp.float32) * 0.5
    return jnp.where(nibble >= 8, -signed_val, signed_val)


def unpack_weights(packed, scaling):
    row_count = packed.shape[0]
    shifts = jnp.arange(8, dtype=jnp.int32) * 4
    nibble = jnp.right_shift(packed[:, :, None], shifts[None, None, :]) & 15
    nibble = nibble.reshape(row_count, packed.shape[1] * 8)
    signed_val = decode_nibble(nibble)
    signed_val = (
        signed_val.reshape(row_count // 32, 32, -1) * scaling.astype(jnp.float32)[:, None, :]
    )
    return signed_val.reshape(row_count, -1).astype(jnp.bfloat16)


def unpack_rows(packed, scaling):
    row_count = packed.shape[0] * 8
    shifts = jnp.arange(8, dtype=jnp.int32) * 4
    nibble = jnp.right_shift(packed[:, None, :], shifts[None, :, None]) & 15
    nibble = nibble.reshape(row_count, packed.shape[1])
    signed_val = decode_nibble(nibble)
    signed_val = (
        signed_val.reshape(row_count // 32, 32, -1) * scaling.astype(jnp.float32)[:, None, :]
    )
    return signed_val.reshape(row_count, -1).astype(jnp.bfloat16)


def rms_normed(hidden, norm_gain):
    widened = hidden.astype(jnp.float32)
    mean_square = jnp.mean(widened * widened, axis=-1, keepdims=True)
    scaled = widened * lax.rsqrt(mean_square + 1e-05) * norm_gain.astype(jnp.float32)
    return scaled.astype(jnp.bfloat16)


def shards(
    hidden,
    route_experts,
    route_weight,
    norm_gain,
    gate_up_codes,
    gate_up_scales,
    gate_up_bias,
    down_codes,
    down_scales,
    down_bias,
):
    ep_count = lax.axis_size("ep")
    tp_count = lax.axis_size("tp")
    tp_rank = lax.axis_index("tp")
    tok_count, model_width = hidden.shape
    top_count = route_experts.shape[1]
    capacity = min(tok_count, max(tp_count, 2 * tok_count * top_count // ep_count))
    normed = rms_normed(hidden, norm_gain)
    flat_routes = route_experts.reshape(-1)
    onehot = (flat_routes[:, None] == jnp.arange(ep_count, dtype=jnp.int32)[None, :]).astype(
        jnp.int32
    )
    before = jnp.cumsum(onehot, axis=0) - onehot
    slot_of = jnp.sum(before * onehot, axis=1)
    target = (flat_routes * capacity + slot_of).reshape(tok_count, top_count)
    columns = jnp.arange(ep_count * capacity, dtype=jnp.int32)
    matches = target[:, :, None] == columns[None, None, :]
    placing = jnp.any(matches, axis=1).astype(jnp.bfloat16)
    weighting = jnp.sum(jnp.where(matches, route_weight[:, :, None], 0.0), axis=1)
    outgoing = lax.dot_general(
        placing, normed, (((0,), (0,)), ((), ())), preferred_element_type=jnp.float32
    ).astype(jnp.bfloat16)
    outgoing = outgoing.reshape(ep_count, capacity, model_width)
    gate_up_weight = unpack_rows(gate_up_codes[0], gate_up_scales[0])
    down_weight = unpack_weights(down_codes[0], down_scales[0])
    arrived = lax.all_to_all(outgoing, "ep", split_axis=0, concat_axis=0, tiled=True)
    source_count, item_count, _ = arrived.shape
    flat_rows = arrived.reshape(source_count * item_count, model_width)
    projected = jnp.dot(
        flat_rows, gate_up_weight, preferred_element_type=jnp.float32
    ) + gate_up_bias[0].astype(jnp.float32)
    gate_part = jnp.minimum(projected[:, 0::2], 7.0)
    upward = jnp.clip(projected[:, 1::2], -7.0, 7.0)
    activated = (gate_part * jax.nn.sigmoid(1.702 * gate_part) * (upward + 1.0)).astype(
        jnp.bfloat16
    )
    partial_value = jnp.dot(activated, down_weight, preferred_element_type=jnp.float32)
    partial_value = partial_value.astype(jnp.bfloat16).astype(jnp.float32)
    partial_value = partial_value.reshape(source_count, item_count, model_width)
    summed = lax.psum_scatter(
        partial_value.astype(jnp.bfloat16), "tp", scatter_dimension=2, tiled=True
    ).astype(jnp.float32)
    answered = (summed + down_bias[0].astype(jnp.float32)).astype(jnp.bfloat16)
    came_back = lax.all_to_all(answered, "ep", split_axis=0, concat_axis=0, tiled=True)
    quarter = model_width // tp_count
    own_cols = lax.dynamic_slice_in_dim(hidden, tp_rank * quarter, quarter, 1).astype(jnp.float32)
    gathered = came_back.reshape(ep_count * capacity, quarter).astype(jnp.float32)
    layer_out = own_cols + jnp.dot(weighting, gathered, precision=lax.Precision.HIGHEST)
    return layer_out.astype(jnp.bfloat16)


def xor_peer(z, d):
    if d & 1:
        z = z + 1 - 2 * (z % 2)
    if d & 2:
        z = z + 2 - 4 * ((z // 2) % 2)
    return z


def layer_kernel(
    sizes,
    hidden,
    routes,
    route_weights,
    gain,
    gate_codes,
    gate_scales_in,
    gate_bias,
    down_codes,
    down_scales_in,
    down_bias,
    out,
    payload,
    gate_scales,
    down_scales,
    rows_in,
    gate_weight,
    down_weight,
    padded_codes,
    activated,
    pair_out,
    pair_in,
    side_out,
    side_in,
    kept,
    far_out,
    far_in,
    own_send,
    own_recv,
    disp_send,
    disp_recv,
    cross_send,
    cross_recv,
    fwd_send,
    fwd_recv,
    pair_send,
    pair_recv,
    side_send,
    side_recv,
    far_send,
    far_recv,
):
    tok, width, n_z = sizes
    half_rows = tok // 2
    half_cols = width // 2
    ep = lax.axis_index("ep")
    x = lax.axis_index("tp")
    z = ep // 2
    core = ep % 2
    partner = {"ep": 2 * z + 1 - core}
    across = {"tp": 1 - x}

    def far(d):
        return {"ep": 2 * xor_peer(z, d) + core}

    def copy(src, dst, send, recv, device):
        return pltpu.make_async_remote_copy(
            src_ref=src,
            dst_ref=dst,
            send_sem=send,
            recv_sem=recv,
            device_id=device,
            device_id_type=pl.DeviceIdType.MESH,
        )

    widened = hidden[...].astype(jnp.float32)
    mean_square = jnp.mean(widened * widened, axis=-1, keepdims=True)
    normed = (widened * lax.rsqrt(mean_square + 1e-05) * gain[...].astype(jnp.float32)).astype(
        jnp.bfloat16
    )
    lane = lax.broadcasted_iota(jnp.int32, (tok, SPARE), 1)
    weight_at = jnp.zeros((tok, SPARE), jnp.float32)
    for k in range(routes.shape[1]):
        chosen = routes[:, k : k + 1] == lane % (2 * n_z)
        weight_at = weight_at + jnp.where(chosen, route_weights[:, k : k + 1], 0.0)
    high = weight_at.astype(jnp.bfloat16).astype(jnp.float32)
    middle = (weight_at - high).astype(jnp.bfloat16).astype(jnp.float32)
    low = weight_at - high - middle
    piece = lane // (2 * n_z)
    spare_lanes = jnp.where(
        piece == 0, high, jnp.where(piece == 1, middle, jnp.where(piece == 2, low, 0.0))
    )
    aligned = width // 128 * 128
    payload[:, :aligned] = normed[:, :aligned]
    payload[:, aligned:] = jnp.concatenate(
        [normed[:, aligned:], spare_lanes.astype(jnp.bfloat16)], axis=1
    )

    barrier = pltpu.get_barrier_semaphore()
    for device in [partner, across] + [far(d) for d in range(1, n_z)]:
        pl.semaphore_signal(
            barrier, inc=1, device_id=device, device_id_type=pl.DeviceIdType.MESH
        )
    pl.semaphore_wait(barrier, n_z + 1)

    def block_rows(owner, half=None):
        if half is None:
            return rows_in.at[pl.ds(pl.multiple_of(owner * tok, tok), tok)]
        start = owner * tok + half * half_rows
        return rows_in.at[pl.ds(pl.multiple_of(start, half_rows), half_rows)]

    own_half = payload.at[pl.ds(pl.multiple_of(x * half_rows, half_rows), half_rows)]
    disp = [
        copy(own_half, block_rows(ep, x), disp_send.at[d], disp_recv.at[d], far(d))
        for d in range(1, n_z)
    ]
    own = copy(payload, block_rows(ep), own_send, own_recv, partner)
    for step in disp:
        step.start()
    own.start()
    rows_in[pl.ds(pl.multiple_of(ep * tok, tok), tok), :] = payload[...]

    def arriving(d, half):
        return block_rows(2 * xor_peer(z, d) + core, half)

    crossing = [
        copy(arriving(d, x), arriving(d, x), cross_send.at[d], cross_recv.at[d], across)
        for d in range(1, n_z)
    ]
    passing = [
        [
            copy(arriving(d, h), arriving(d, h), fwd_send.at[d, i], fwd_recv.at[d, i], partner)
            for i, h in enumerate((x, 1 - x))
        ]
        for d in range(1, n_z)
    ]

    def pass_on(d):
        disp[d - 1].wait_recv()
        crossing[d - 1].start()
        passing[d - 1][0].start()

    def pass_crossed(d):
        crossing[d - 1].wait_recv()
        passing[d - 1][1].start()

    gate_scales[...] = gate_scales_in[...].astype(jnp.float32) * 0.5
    scale_rows, scale_lanes = down_scales_in.shape[0], down_scales.shape[1]
    down_scales[:, scale_lanes - 128 :] = jnp.zeros((2 * scale_rows, 128), jnp.float32)
    for h in range(2):
        down_scales[h * scale_rows : (h + 1) * scale_rows, :half_cols] = (
            down_scales_in[:, h * half_cols : (h + 1) * half_cols].astype(jnp.float32) * 0.5
        )
    place = lax.broadcasted_iota(jnp.int32, (8, 1), 0) * 4
    gate_cols = gate_codes.shape[1]
    col_step = 512 if gate_cols % 512 == 0 else 256

    def gate_rows(s, carry):
        base = pl.multiple_of(s * 8, 8)
        for col in range(0, gate_cols, col_step):
            words = gate_codes[pl.ds(base, 8), col : col + col_step]
            shifted = words
            for group in range(2):
                scale = jnp.broadcast_to(
                    gate_scales[pl.ds(2 * s + group, 1), col : col + col_step], (8, col_step)
                )
                pieces = []
                for w in range(4):
                    row = group * 4 + w
                    one = jnp.broadcast_to(shifted[row : row + 1, :], (8, col_step))
                    place_wide = jnp.broadcast_to(place, (8, col_step))
                    quad = jnp.left_shift(lax.shift_right_logical(one, place_wide), 2) & 28
                    doubled = lax.shift_right_logical(jnp.full_like(one, MAGNITUDES), quad) & 15
                    negative = jnp.left_shift(one, 28 - place_wide) < 0
                    pieces.append(
                        doubled.astype(jnp.float32) * jnp.where(negative, -scale, scale)
                    )
                start = pl.multiple_of(s * 64 + group * 32, 32)
                gate_weight[pl.ds(start, 32), col : col + col_step] = jnp.concatenate(
                    pieces, axis=0
                ).astype(jnp.bfloat16)
        return carry

    gate_steps = gate_codes.shape[0] // 8
    gate_weight[pl.ds(width, SPARE), :] = jnp.zeros((SPARE, gate_cols), jnp.bfloat16)
    cut = gate_steps // 2
    lax.fori_loop(0, cut, gate_rows, 0)
    pass_on(1)
    lax.fori_loop(cut, gate_steps, gate_rows, 0)
    pass_on(2)
    pass_crossed(1)

    code_words = down_codes.shape[1]
    whole_lanes = code_words // 128 * 128
    lane_total = padded_codes.shape[1]
    padded_codes[:, lane_total - 128 :] = jnp.zeros((padded_codes.shape[0], 128), jnp.int32)
    padded_codes[:, 0:whole_lanes] = down_codes[:, 0:whole_lanes]
    padded_codes[:, whole_lanes:code_words] = down_codes[:, whole_lanes:code_words]
    lanes = lax.broadcasted_iota(jnp.int32, (32, 128), 1)
    lane_word = lanes // 8
    lane_place = (lanes % 8) * 4
    lane_sign = 28 - lane_place

    down_steps = down_codes.shape[0] // 32

    def down_rows(h, s, carry):
        base = pl.multiple_of(s * 32, 32)
        sources = [
            padded_codes[pl.ds(base, 32), v * 128 : (v + 1) * 128] for v in range(lane_total // 128)
        ]
        scale_row = down_scales[pl.ds(h * down_steps + s, 1), :]
        for b in range(-(-half_cols // 128)):
            first = h * (half_cols // 8) + 16 * b
            low, high = first // 128, (first + 15) // 128
            index = (lane_word + first % 128) % 128
            words = jnp.take_along_axis(sources[low], index, axis=1, mode="promise_in_bounds")
            if high != low:
                other = jnp.take_along_axis(sources[high], index, axis=1, mode="promise_in_bounds")
                words = jnp.where(lane_word + first % 128 < 128, words, other)
            size = min(128, half_cols - 128 * b)
            scale = jnp.broadcast_to(scale_row[:, 128 * b : 128 * (b + 1)], (32, 128))
            quad = jnp.left_shift(lax.shift_right_logical(words, lane_place), 2) & 28
            doubled = lax.shift_right_logical(jnp.full_like(words, MAGNITUDES), quad) & 15
            negative = jnp.left_shift(words, lane_sign) < 0
            value = (doubled.astype(jnp.float32) * jnp.where(negative, -scale, scale)).astype(
                jnp.bfloat16
            )
            down_weight[h, pl.ds(base, 32), 128 * b : 128 * b + size] = value[:, :size]
        return carry

    lax.fori_loop(0, down_steps, functools.partial(down_rows, 0), 0)
    pass_on(3)
    pass_crossed(2)
    lax.fori_loop(0, down_steps, functools.partial(down_rows, 1), 0)
    pass_crossed(3)

    picks = (
        lax.broadcasted_iota(jnp.int32, (256, 128), 0)
        == 2 * lax.broadcasted_iota(jnp.int32, (256, 128), 1)
    ).astype(jnp.float32).astype(jnp.bfloat16)

    def gate_tile(t, carry):
        cols = pl.ds(pl.multiple_of(t * 256, 256), 256)
        projected = jnp.dot(
            rows_in[...], gate_weight[:, cols], preferred_element_type=jnp.float32
        ) + gate_bias[:, cols].astype(jnp.float32)
        gate_part = jnp.minimum(projected, 7.0)
        upward = pltpu.roll(jnp.clip(projected, -7.0, 7.0), 255, 1)
        value = gate_part * jax.nn.sigmoid(1.702 * gate_part) * (upward + 1.0)
        activated[:, pl.ds(pl.multiple_of(t * 128, 128), 128)] = jnp.dot(
            value.astype(jnp.bfloat16), picks, preferred_element_type=jnp.float32
        ).astype(jnp.bfloat16)
        return carry


    tail = lax.broadcasted_iota(jnp.int32, (2 * tok, SPARE), 1)
    pairing = [
        copy(pair_out.at[d], pair_in.at[d], pair_send.at[d], pair_recv.at[d], partner)
        for d in range(n_z)
    ]
    siding = [
        copy(side_out.at[d], side_in.at[d], side_send.at[d], side_recv.at[d], across)
        for d in range(n_z)
    ]
    faring = [
        None if d == 0 else copy(far_out.at[d], far_in.at[d], far_send.at[d], far_recv.at[d], far(d))
        for d in range(n_z)
    ]

    def multiply(d):
        start = pl.multiple_of(xor_peer(z, d) * 2 * tok, 2 * tok)
        rows = activated[pl.ds(start, 2 * tok), :]
        spare = rows_in[pl.ds(start, 2 * tok), width:].astype(jnp.float32)
        hit = (tail == ep) | (tail == ep + 2 * n_z) | (tail == ep + 4 * n_z)
        weight = jnp.sum(jnp.where(hit, spare, 0.0), axis=1, keepdims=True)
        for h in range(2):
            added = down_bias[...].astype(jnp.float32) * jnp.where(x == h, 1.0, 0.0)
            value = jnp.dot(rows, down_weight[h], preferred_element_type=jnp.float32) + added
            value = value * weight
            first, second = value[:tok], value[tok:]
            pair_out[d, h] = jnp.where(core == 0, second, first).astype(jnp.bfloat16)
            kept[d, h] = jnp.where(core == 0, first, second).astype(jnp.bfloat16)
        pairing[d].start()

    def fold_pair(d):
        pairing[d].wait_recv()
        sums = [
            kept[d, h].astype(jnp.float32) + pair_in[d, h].astype(jnp.float32) for h in range(2)
        ]
        side_out[d] = jnp.where(x == 0, sums[1], sums[0]).astype(jnp.bfloat16)
        kept[d, 0] = jnp.where(x == 0, sums[0], sums[1]).astype(jnp.bfloat16)
        siding[d].start()

    def fold_side(d):
        siding[d].wait_recv()
        total = kept[d, 0].astype(jnp.float32) + side_in[d].astype(jnp.float32)
        if d == 0:
            return total
        far_out[d] = total.astype(jnp.bfloat16)
        faring[d].start()
        return None

    def gathered(d):
        for step in passing[d - 1]:
            step.wait_recv()

    own.wait_recv()
    for d in range(1, n_z):
        gathered(d)
    lax.fori_loop(0, gate_cols // 256, gate_tile, 0)
    multiply(3)
    multiply(2)
    fold_pair(3)
    multiply(1)
    fold_pair(2)
    fold_side(3)
    multiply(0)
    fold_pair(1)
    fold_side(2)
    fold_pair(0)
    fold_side(1)
    own_cols = jnp.where(x == 0, hidden[:, :half_cols], hidden[:, half_cols:])
    total = fold_side(0) + own_cols.astype(jnp.float32)
    for d in (1, 3, 2):
        faring[d].wait_recv()
        total = total + far_in[d].astype(jnp.float32)
    out[...] = total.astype(jnp.bfloat16)

    own.wait_send()
    for d in range(1, n_z):
        disp[d - 1].wait_send()
        crossing[d - 1].wait_send()
        for step in passing[d - 1]:
            step.wait_send()
        faring[d].wait_send()
    for d in range(n_z):
        pairing[d].wait_send()
        siding[d].wait_send()


def dense_shards(
    hidden,
    route_experts,
    route_weight,
    norm_gain,
    gate_up_codes,
    gate_up_scales,
    gate_up_bias,
    down_codes,
    down_scales,
    down_bias,
):
    ep_count = lax.axis_size("ep")
    tok, width = hidden.shape
    n_z = ep_count // 2
    half = width // 2
    units = down_codes.shape[1]
    lanes = -(-half // 128) * 128
    code_lanes = -(-down_codes.shape[2] // 128) * 128
    bf16 = jnp.bfloat16
    dma = pltpu.SemaphoreType.DMA
    vmem = pltpu.VMEM
    return pl.pallas_call(
        functools.partial(layer_kernel, (tok, width, n_z)),
        out_shape=jax.ShapeDtypeStruct((tok, half), bf16),
        in_specs=[pl.BlockSpec(memory_space=vmem)] * 10,
        out_specs=pl.BlockSpec(memory_space=vmem),
        scratch_shapes=[
            vmem((tok, width + SPARE), bf16),
            vmem(gate_up_scales.shape[1:], jnp.float32),
            vmem((2 * down_scales.shape[1], lanes), jnp.float32),
            vmem((ep_count * tok, width + SPARE), bf16),
            vmem((width + SPARE, gate_up_codes.shape[2]), bf16),
            vmem((2, units, half), bf16),
            vmem((units, code_lanes), jnp.int32),
            vmem((ep_count * tok, units), bf16),
            vmem((n_z, 2, tok, half), bf16),
            vmem((n_z, 2, tok, half), bf16),
            vmem((n_z, tok, half), bf16),
            vmem((n_z, tok, half), bf16),
            vmem((n_z, 2, tok, half), bf16),
            vmem((n_z, tok, half), bf16),
            vmem((n_z, tok, half), bf16),
            dma,
            dma,
            dma((n_z,)),
            dma((n_z,)),
            dma((n_z,)),
            dma((n_z,)),
            dma((n_z, 2)),
            dma((n_z, 2)),
            dma((n_z,)),
            dma((n_z,)),
            dma((n_z,)),
            dma((n_z,)),
            dma((n_z,)),
            dma((n_z,)),
        ],
        compiler_params=pltpu.CompilerParams(
            collective_id=0, has_side_effects=True, vmem_limit_bytes=63 * 1024 * 1024
        ),
    )(
        hidden,
        route_experts,
        route_weight,
        norm_gain.reshape(1, width),
        gate_up_codes[0],
        gate_up_scales[0],
        gate_up_bias,
        down_codes[0],
        down_scales[0],
        down_bias,
    )


def solution(mesh):
    def layer(*arrays):
        tok, top = arrays[1].shape
        ep_count, tp_count = lax.axis_size("ep"), lax.axis_size("tp")
        dense = 2 * top >= ep_count and tp_count == 2 and ep_count == 8
        return (dense_shards if dense else shards)(*arrays)

    placed = (
        P(("groups", "ep"), None),
        P(("groups", "ep"), None),
        P(("groups", "ep"), None),
        P(),
        P("ep", None, "tp"),
        P("ep", None, "tp"),
        P("ep", "tp"),
        P("ep", "tp", None),
        P("ep", "tp", None),
        P("ep", "tp"),
    )
    return jax.shard_map(
        layer, mesh=mesh, in_specs=placed, out_specs=P(("groups", "ep"), "tp"), check_vma=False
    )
```

profile of v0, /device:TPU:0, one launch (start us, length us, event | category | flops | bytes accessed | tf_op | source)
XLA Modules:
  0.0 86.7 jit_solution(12421087605635957735)
XLA Ops:
  0.0 1.3 %reshape.3.gain = bf16[1,2880]{1,0:T(2,128)(2,1)} reshape(bf16[2880]{0:T(1024)(128)(2,1)} %param.13) | data formatting | bytes 11520 | tf_op jit(solution)/shard_map/reshape | solution.py:519
  1.3 1.4 %copy.12.routes = s32[64,4]{1,0:T(8,128)} copy(s32[64,4]{0,1:T(4,128)} %param.11) | data formatting | bytes 2048 | tf_op args[1]
  2.7 1.4 %copy.13.route_weights = f32[64,4]{1,0:T(8,128)} copy(f32[64,4]{0,1:T(4,128)} %param.12) | data formatting | bytes 2048 | tf_op args[2]
  4.0 2.8 %copy.11 = s32[1,1280,360]{2,1,0:T(8,128)} copy(s32[1,1280,360]{1,2,0:T(8,128)} %param.17) | data formatting | bytes 3686400 | tf_op args[7]
  6.9 78.2 %shard_map.100 = bf16[64,1440]{1,0:T(8,128)(2,1)} custom-call(bf16[64,2880]{1,0:T(8,128)(2,1)} %hidden.1, s32[64,4]{1,0:T(8,128)} %copy.12.routes, f32[64,4]{1,0:T(8,128)} %copy.13.route_weights, bf16[1,2880]{1,0:T(2,128)(2,1)} %reshape.3.gain, s32[360,2560]{1,0:T(8,128)} %bitcast.5, bf16[90,2560]{1,0:T(8,128)(2,1)} %bitcast.6, bf16[1,2560]{1,0:T(2,128)(2,1)} %gate_bias.1, ...), custom_call_target="tpu_custom_call" | custom-call | tf_op jit(solution)/shard_map/pallas_call | solution.py:476
  85.1 1.6 %copy.15 = bf16[64,1440]{1,0:T(8,128)(2,1)} copy(bf16[64,1440]{1,0:T(8,128)(2,1)} %shard_map.100) | data formatting | bytes 368640
where the time goes:
time: 86.9 us; the launch traced here: 86.7 us
  Pallas kernels  78.2 us (90%)
  local copies, waits for them, and re-layouts  8.51 us (10%)
    pallas_call x1, Pallas kernels, dense_shards(): pl.pallas_call(functools.partial(layer_kernel, (tok, width, n_z)), out_sh...  78.2 us
    unnamed x4, local copies, waits for them, and re-layouts  7.21 us

commit v1 on v0

v1 whole, which is shorter than its diff:
```python
import functools

import jax
import jax.numpy as jnp
from jax import lax
from jax.experimental import pallas as pl
from jax.experimental.pallas import tpu as pltpu
from jax.sharding import PartitionSpec as P

MAGNITUDES = 0xC8643210 - (1 << 32)
SPARE = 64


def decode_nibble(nibble):
    magnit = nibble & 7
    exponent = jnp.maximum(jnp.right_shift(magnit, 1) - 1, 0)
    doubled = jnp.where(magnit < 2, magnit, jnp.left_shift(2 + (magnit & 1), exponent))
    signed_val = doubled.astype(jnp.float32) * 0.5
    return jnp.where(nibble >= 8, -signed_val, signed_val)


def unpack_weights(packed, scaling):
    row_count = packed.shape[0]
    shifts = jnp.arange(8, dtype=jnp.int32) * 4
    nibble = jnp.right_shift(packed[:, :, None], shifts[None, None, :]) & 15
    nibble = nibble.reshape(row_count, packed.shape[1] * 8)
    signed_val = decode_nibble(nibble)
    signed_val = (
        signed_val.reshape(row_count // 32, 32, -1) * scaling.astype(jnp.float32)[:, None, :]
    )
    return signed_val.reshape(row_count, -1).astype(jnp.bfloat16)


def unpack_rows(packed, scaling):
    row_count = packed.shape[0] * 8
    shifts = jnp.arange(8, dtype=jnp.int32) * 4
    nibble = jnp.right_shift(packed[:, None, :], shifts[None, :, None]) & 15
    nibble = nibble.reshape(row_count, packed.shape[1])
    signed_val = decode_nibble(nibble)
    signed_val = (
        signed_val.reshape(row_count // 32, 32, -1) * scaling.astype(jnp.float32)[:, None, :]
    )
    return signed_val.reshape(row_count, -1).astype(jnp.bfloat16)


def rms_normed(hidden, norm_gain):
    widened = hidden.astype(jnp.float32)
    mean_square = jnp.mean(widened * widened, axis=-1, keepdims=True)
    scaled = widened * lax.rsqrt(mean_square + 1e-05) * norm_gain.astype(jnp.float32)
    return scaled.astype(jnp.bfloat16)


def shards(
    hidden,
    route_experts,
    route_weight,
    norm_gain,
    gate_up_codes,
    gate_up_scales,
    gate_up_bias,
    down_codes,
    down_scales,
    down_bias,
):
    ep_count = lax.axis_size("ep")
    tp_count = lax.axis_size("tp")
    tp_rank = lax.axis_index("tp")
    tok_count, model_width = hidden.shape
    top_count = route_experts.shape[1]
    capacity = min(tok_count, max(tp_count, 2 * tok_count * top_count // ep_count))
    normed = rms_normed(hidden, norm_gain)
    flat_routes = route_experts.reshape(-1)
    onehot = (flat_routes[:, None] == jnp.arange(ep_count, dtype=jnp.int32)[None, :]).astype(
        jnp.int32
    )
    before = jnp.cumsum(onehot, axis=0) - onehot
    slot_of = jnp.sum(before * onehot, axis=1)
    target = (flat_routes * capacity + slot_of).reshape(tok_count, top_count)
    columns = jnp.arange(ep_count * capacity, dtype=jnp.int32)
    matches = target[:, :, None] == columns[None, None, :]
    placing = jnp.any(matches, axis=1).astype(jnp.bfloat16)
    weighting = jnp.sum(jnp.where(matches, route_weight[:, :, None], 0.0), axis=1)
    outgoing = lax.dot_general(
        placing, normed, (((0,), (0,)), ((), ())), preferred_element_type=jnp.float32
    ).astype(jnp.bfloat16)
    outgoing = outgoing.reshape(ep_count, capacity, model_width)
    gate_up_weight = unpack_rows(gate_up_codes[0], gate_up_scales[0])
    down_weight = unpack_weights(down_codes[0], down_scales[0])
    arrived = lax.all_to_all(outgoing, "ep", split_axis=0, concat_axis=0, tiled=True)
    source_count, item_count, _ = arrived.shape
    flat_rows = arrived.reshape(source_count * item_count, model_width)
    projected = jnp.dot(
        flat_rows, gate_up_weight, preferred_element_type=jnp.float32
    ) + gate_up_bias[0].astype(jnp.float32)
    gate_part = jnp.minimum(projected[:, 0::2], 7.0)
    upward = jnp.clip(projected[:, 1::2], -7.0, 7.0)
    activated = (gate_part * jax.nn.sigmoid(1.702 * gate_part) * (upward + 1.0)).astype(
        jnp.bfloat16
    )
    partial_value = jnp.dot(activated, down_weight, preferred_element_type=jnp.float32)
    partial_value = partial_value.astype(jnp.bfloat16).astype(jnp.float32)
    partial_value = partial_value.reshape(source_count, item_count, model_width)
    summed = lax.psum_scatter(
        partial_value.astype(jnp.bfloat16), "tp", scatter_dimension=2, tiled=True
    ).astype(jnp.float32)
    answered = (summed + down_bias[0].astype(jnp.float32)).astype(jnp.bfloat16)
    came_back = lax.all_to_all(answered, "ep", split_axis=0, concat_axis=0, tiled=True)
    quarter = model_width // tp_count
    own_cols = lax.dynamic_slice_in_dim(hidden, tp_rank * quarter, quarter, 1).astype(jnp.float32)
    gathered = came_back.reshape(ep_count * capacity, quarter).astype(jnp.float32)
    layer_out = own_cols + jnp.dot(weighting, gathered, precision=lax.Precision.HIGHEST)
    return layer_out.astype(jnp.bfloat16)

BF16 = jnp.bfloat16
F32 = jnp.float32
CHUNKS = 2


def word_order(size, lone):
    pos = lax.broadcasted_iota(jnp.int32, (size, size), 1)
    col = lax.broadcasted_iota(jnp.int32, (size, size), 0)
    inner = pos & 63
    source = pos - inner + 8 * (inner & 7) + (inner >> 3)
    if lone:
        last = pos - (size - 32)
        half = size - 32 + 8 * (last & 3) + 2 * (last >> 3) + ((last & 7) >> 2)
        source = jnp.where(last >= 0, half, source)
    return (col == source).astype(F32).astype(BF16)


def matmul(a, b, contract=(1, 0)):
    return lax.dot_general(
        a, b, (((contract[0],), (contract[1],)), ((), ())), preferred_element_type=F32
    )


def column_blocks(total):
    blocks = [(start, 256) for start in range(0, total - total % 256, 256)]
    return blocks + ([(total // 256 * 256, total % 256)] if total % 256 else [])


def decoded(words, quad, negative, scale):
    doubled = lax.shift_right_logical(jnp.full_like(words, MAGNITUDES), quad) & 15
    return doubled.astype(F32) * jnp.where(negative, -scale, scale)


def decode_words(words, scales):
    pieces = []
    for j in range(8):
        moved = jnp.left_shift(words, 2) if j == 0 else lax.shift_right_logical(words, 4 * j - 2)
        negative = (words if j == 7 else jnp.left_shift(words, 28 - 4 * j)) < 0
        pieces.append(decoded(words, moved & 28, negative, scales[j]))
    return jnp.concatenate(pieces, axis=0).astype(BF16)


def layer_kernel(
    sizes,
    hidden,
    routes,
    route_weights,
    gain,
    gate_codes_in,
    gate_scales_in,
    gate_bias,
    down_codes_in,
    down_scales_in,
    down_bias,
    out,
    gate_codes,
    down_codes,
    shifted_codes,
    gate_scales,
    down_scales,
    own_part,
    bias_part,
    rows_in,
    gate_weight,
    down_weight,
    activated,
    pair_out,
    pair_in,
    side_out,
    side_in,
    kept,
    step_out,
    step_in,
    load_sem,
    own_send,
    own_recv,
    line_send,
    line_recv,
    cross_send,
    cross_recv,
    pass_send,
    pass_recv,
    pair_send,
    pair_recv,
    side_send,
    side_recv,
    step_send,
    step_recv,
):
    tok, width, n_z, cuts = sizes
    half_rows = tok // 2
    part_rows = half_rows // CHUNKS
    half_cols = width // 2
    ep = lax.axis_index("ep")
    x = lax.axis_index("tp")
    z = ep // 2
    core = ep % 2
    partner = {"ep": 2 * z + 1 - core}
    across = {"tp": 1 - x}
    beside = z + 1 - 2 * (z % 2)
    beyond = (z + 2) % 4
    neighbour = {"ep": 2 * beside + core}
    opposite = {"ep": 2 * beyond + core}
    along = [{"ep": 2 * ((z + 1) % n_z) + core}, {"ep": 2 * ((z + n_z - 1) % n_z) + core}]

    def copy(src, dst, send, recv, device):
        return pltpu.make_async_remote_copy(
            src_ref=src,
            dst_ref=dst,
            send_sem=send,
            recv_sem=recv,
            device_id=device,
            device_id_type=pl.DeviceIdType.MESH,
        )

    loads = [
        pltpu.make_async_copy(gate_codes_in, gate_codes, load_sem.at[0]),
        pltpu.make_async_copy(down_codes_in, down_codes, load_sem.at[1]),
    ]
    for load in loads:
        load.start()
    barrier = pltpu.get_barrier_semaphore()
    others = [{"ep": 2 * ((z + d) % n_z) + core} for d in range(1, n_z)]
    for device in [partner, across] + others:
        pl.semaphore_signal(
            barrier, inc=1, device_id=device, device_id_type=pl.DeviceIdType.MESH
        )

    order = word_order(256, False)
    blocks = column_blocks(width)
    wide = jnp.concatenate(
        [matmul(hidden[:, c : c + n], order[:n, :n]) for c, n in blocks], axis=1
    )
    gain_row = jnp.concatenate(
        [matmul(gain[:, c : c + n], order[:n, :n]) for c, n in blocks], axis=1
    )
    plain = hidden[...].astype(F32)
    mean_square = jnp.mean(plain * plain, axis=-1, keepdims=True)
    normed = (wide * lax.rsqrt(mean_square + 1e-05) * gain_row).astype(BF16)
    number = lax.broadcasted_iota(jnp.int32, (SPARE, tok), 0)
    weight_at = jnp.zeros((SPARE, tok), F32)
    for k in range(routes.shape[0]):
        chosen = routes[k : k + 1, :] == number % (2 * n_z)
        weight_at = weight_at + jnp.where(chosen, route_weights[k : k + 1, :], 0.0)
    high = weight_at.astype(BF16).astype(F32)
    middle = (weight_at - high).astype(BF16).astype(F32)
    low = weight_at - high - middle
    piece = number // (2 * n_z)
    spare = jnp.where(
        piece == 0, high, jnp.where(piece == 1, middle, jnp.where(piece == 2, low, 0.0))
    )
    same = lax.broadcasted_iota(jnp.int32, (tok, tok), 0) == lax.broadcasted_iota(
        jnp.int32, (tok, tok), 1
    )
    spare_lanes = matmul(same.astype(F32).astype(BF16), spare.astype(BF16), (1, 1))
    aligned = width // 128 * 128
    mine = pl.ds(pl.multiple_of(ep * tok, tok), tok)
    rows_in[mine, :aligned] = normed[:, :aligned]
    rows_in[mine, aligned:] = jnp.concatenate(
        [normed[:, aligned:], spare_lanes.astype(BF16)], axis=1
    )

    pl.semaphore_wait(barrier, n_z + 1)

    def part(chip, half, k):
        start = (2 * chip + core) * tok + half * half_rows + k * part_rows
        return rows_in.at[pl.ds(pl.multiple_of(start, part_rows), part_rows)]

    def line_copy(side, s, k, chip):
        return copy(
            part(chip, x, k),
            part(chip, x, k),
            line_send.at[side, s, k],
            line_recv.at[side, s, k],
            along[side],
        )

    def origin(side, s):
        return (z + n_z - s) % n_z if side == 0 else (z + s) % n_z

    def has(side, s):
        return z >= s if side == 0 else z + s < n_z

    def goes(side):
        return z < n_z - 1 if side == 0 else z > 0

    def both(side, s):
        return (z >= s) & (z < n_z - 1) if side == 0 else (z + s < n_z) & (z > 0)

    for k in range(CHUNKS):
        for side in range(2):

            @pl.when(goes(side))
            def _():
                line_copy(side, 1, k, z).start()

    own_block = rows_in.at[mine]
    own = copy(own_block, own_block, own_send, own_recv, partner)
    own.start()

    def cross_copy(side, s, k):
        ref = part(origin(side, s), x, k)
        return copy(ref, ref, cross_send.at[side, s, k], cross_recv.at[side, s, k], across)

    def pass_copy(side, s, k, i):
        ref = part(origin(side, s), x if i == 0 else 1 - x, k)
        return copy(ref, ref, pass_send.at[side, s, k, i], pass_recv.at[side, s, k, i], partner)

    def arrive(s, k):
        for side in range(2):

            @pl.when(has(side, s))
            def _():
                line_copy(side, s, k, origin(side, s)).wait_recv()
                if s < n_z - 1:

                    @pl.when(goes(side))
                    def _():
                        line_copy(side, s + 1, k, origin(side, s)).start()

                cross_copy(side, s, k).start()
                pass_copy(side, s, k, 0).start()

    def arrive_crossed(s, k):
        for side in range(2):

            @pl.when(has(side, s))
            def _():
                cross_copy(side, s, k).wait_recv()
                pass_copy(side, s, k, 1).start()

    def complete(s):
        for side in range(2):

            @pl.when(has(side, s))
            def _():
                for k in range(CHUNKS):
                    for i in range(2):
                        pass_copy(side, s, k, i).wait_recv()

    def drain(s):
        for side in range(2):

            @pl.when(has(side, s))
            def _():
                for k in range(CHUNKS):
                    cross_copy(side, s, k).wait_send()
                    for i in range(2):
                        pass_copy(side, s, k, i).wait_send()
                    if s < n_z - 1:

                        @pl.when(goes(side))
                        def _():
                            line_copy(side, s + 1, k, origin(side, s)).wait_send()

    gate_scales[...] = gate_scales_in[...].astype(F32) * 0.5
    gate_cols = gate_codes.shape[1]
    col_step = 512 if gate_cols % 512 == 0 else 256
    upper = lax.broadcasted_iota(jnp.int32, (8, col_step), 0) < 4

    def gate_rows(s, carry):
        base = pl.multiple_of(s * 8, 8)
        for col in range(0, gate_cols, col_step):
            words = gate_codes[pl.ds(base, 8), col : col + col_step]
            first, second = (
                jnp.broadcast_to(
                    gate_scales[pl.ds(2 * s + i, 1), col : col + col_step], (8, col_step)
                )
                for i in range(2)
            )
            scale = jnp.where(upper, first, second)
            gate_weight[pl.ds(pl.multiple_of(s * 64, 64), 64), col : col + col_step] = (
                decode_words(words, [scale] * 8)
            )
        return carry

    gate_steps = gate_codes.shape[0] // 8
    gate_weight[pl.ds(width, SPARE), :] = jnp.zeros((SPARE, gate_cols), BF16)
    loads[0].wait()
    marks = [0, 12, 23, 34, gate_steps]
    services = [
        lambda: arrive(1, 0),
        lambda: arrive(1, 1),
        lambda: (arrive(2, 0), arrive_crossed(1, 0)),
        lambda: (arrive(2, 1), arrive_crossed(1, 1)),
    ]
    for low_mark, high_mark, service in zip(marks[:-1], marks[1:], services):
        lax.fori_loop(low_mark, high_mark, gate_rows, 0)
        service()

    scale_rows = down_scales_in.shape[0]
    half_blocks = column_blocks(half_cols)
    tail_size = half_blocks[-1][1]
    tail_order = word_order(tail_size, True)
    for h in range(2):
        for c, n in half_blocks:
            picked = tail_order if n == tail_size else order
            block = down_scales_in[:, h * half_cols + c : h * half_cols + c + n]
            down_scales[h, c : c + n, :scale_rows] = matmul(picked, block, (0, 1)).astype(BF16)
    shown = jnp.where(x == 0, hidden[:, :half_cols], hidden[:, half_cols:])
    for c, n in half_blocks:
        picked = tail_order if n == tail_size else order
        own_part[:, c : c + n] = matmul(shown[:, c : c + n], picked)
        bias_part[:, c : c + n] = matmul(down_bias[:, c : c + n], picked)

    units = down_codes.shape[1]
    words_half = half_cols // 8
    down_steps = words_half // 8
    spread = (
        lax.broadcasted_iota(jnp.int32, (scale_rows, units), 1) // 32
        == lax.broadcasted_iota(jnp.int32, (scale_rows, units), 0)
    ).astype(F32) * 0.5
    spread = spread.astype(BF16)
    loads[1].wait()
    shifted_codes[...] = down_codes[words_half : words_half + down_steps * 8, :]

    def down_rows(h, g, carry):
        base = pl.multiple_of(g * 64, 64)
        source = down_codes if h == 0 else shifted_codes
        start = pl.multiple_of(g * 8, 8)
        scale_block = down_scales[h, pl.ds(base, 64), :scale_rows]
        for col in range(0, units, 256):
            scale = matmul(scale_block, spread[:, col : col + 256])
            words = source[pl.ds(start, 8), col : col + 256]
            down_weight[h, pl.ds(base, 64), col : col + 256] = decode_words(
                words, [scale[8 * j : 8 * j + 8] for j in range(8)]
            )
        return carry

    place = (lax.broadcasted_iota(jnp.int32, (8, units), 0) >> 2) * 4

    def down_last(h):
        base = down_steps * 64
        four = down_codes[h * words_half + down_steps * 8 : (h + 1) * words_half, :]
        words = jnp.concatenate([four, four], axis=0)
        scale = matmul(down_scales[h, base : base + 32, :scale_rows], spread)
        pieces = []
        for i in range(4):
            shift = place + 8 * i
            quad = jnp.left_shift(lax.shift_right_logical(words, shift), 2) & 28
            negative = jnp.left_shift(words, 28 - shift) < 0
            pieces.append(decoded(words, quad, negative, scale[8 * i : 8 * i + 8]))
        down_weight[h, base : base + 32, :] = jnp.concatenate(pieces, axis=0).astype(BF16)

    middle_step = down_steps // 2
    lax.fori_loop(0, middle_step, functools.partial(down_rows, 0), 0)
    arrive(3, 0)
    lax.fori_loop(middle_step, down_steps, functools.partial(down_rows, 0), 0)
    arrive_crossed(2, 0)
    arrive(3, 1)
    lax.fori_loop(0, middle_step, functools.partial(down_rows, 1), 0)
    arrive_crossed(2, 1)
    lax.fori_loop(middle_step, down_steps, functools.partial(down_rows, 1), 0)
    down_last(0)
    down_last(1)
    arrive_crossed(3, 0)
    arrive_crossed(3, 1)

    picks = (
        lax.broadcasted_iota(jnp.int32, (256, 128), 0)
        == 2 * lax.broadcasted_iota(jnp.int32, (256, 128), 1)
    ).astype(F32).astype(BF16)
    batch_rows = 4 * tok
    near = z // 2
    place_in = z % 2
    starts = [pl.multiple_of((1 - near) * batch_rows, batch_rows),
              pl.multiple_of(near * batch_rows, batch_rows)]

    def gate_tile(b, t, carry):
        cols = pl.ds(pl.multiple_of(t * 256, 256), 256)
        projected = jnp.dot(
            rows_in[pl.ds(starts[b], batch_rows), :],
            gate_weight[:, cols],
            preferred_element_type=F32,
        ) + gate_bias[:, cols].astype(F32)
        gate_part = jnp.minimum(projected, 7.0)
        upward = pltpu.roll(jnp.clip(projected, -7.0, 7.0), 255, 1)
        value = gate_part * jax.nn.sigmoid(1.702 * gate_part) * (upward + 1.0)
        activated[b, :, pl.ds(pl.multiple_of(t * 128, 128), 128)] = jnp.dot(
            value.astype(BF16), picks, preferred_element_type=F32
        ).astype(BF16)
        return carry

    def sections(ref, b, h, q):
        c, n = cuts[q]
        return ref.at[b, h, :, :, pl.ds(c, n)]

    def pair_copy(b, h, q):
        return copy(
            sections(pair_out, b, h, q),
            sections(pair_in, b, h, q),
            pair_send.at[b, h, q],
            pair_recv.at[b, h, q],
            partner,
        )

    def side_copy(b, q):
        c, n = cuts[q]
        return copy(
            side_out.at[b, :, :, pl.ds(c, n)],
            side_in.at[b, :, :, pl.ds(c, n)],
            side_send.at[b, q],
            side_recv.at[b, q],
            across,
        )

    def step_copy(i, q):
        c, n = cuts[q]
        return copy(
            step_out.at[i, :, pl.ds(c, n)],
            step_in.at[i, :, pl.ds(c, n)],
            step_send.at[i, q],
            step_recv.at[i, q],
            opposite if i == 1 else neighbour,
        )

    tail = lax.broadcasted_iota(jnp.int32, (batch_rows, SPARE), 1)

    def weights_of(b):
        extra = rows_in[pl.ds(starts[b], batch_rows), width:].astype(F32)
        hit = (tail == ep) | (tail == ep + 2 * n_z) | (tail == ep + 4 * n_z)
        return jnp.sum(jnp.where(hit, extra, 0.0), axis=1, keepdims=True)

    def multiply(b, h, q, weight):
        c, n = cuts[q]
        which = 1 - x if h == 0 else x
        value = matmul(activated[b], down_weight[which, c : c + n, :], (1, 1))
        if h == 1:
            value = value + bias_part[:, c : c + n]
        value = value * weight
        for i in range(2):
            first = value[2 * i * tok : (2 * i + 1) * tok]
            second = value[(2 * i + 1) * tok : (2 * i + 2) * tok]
            pair_out[b, h, i, :, c : c + n] = jnp.where(core == 0, second, first).astype(BF16)
            kept[b, h, i, :, c : c + n] = jnp.where(core == 0, first, second).astype(BF16)
        pair_copy(b, h, q).start()

    def fold_pair(b, h, q):
        c, n = cuts[q]
        pair_copy(b, h, q).wait_recv()
        total = kept[b, h, :, :, c : c + n].astype(F32) + pair_in[
            b, h, :, :, c : c + n
        ].astype(F32)
        if h == 0:
            side_out[b, :, :, c : c + n] = total.astype(BF16)
            side_copy(b, q).start()
        else:
            kept[b, h, :, :, c : c + n] = total.astype(BF16)

    def folded(b, i, q):
        c, n = cuts[q]
        return kept[b, 1, i, :, c : c + n].astype(F32) + side_in[b, i, :, c : c + n].astype(F32)

    def fold_side(b, q):
        c, n = cuts[q]
        side_copy(b, q).wait_recv()
        step_out[0 if b == 0 else 2, :, c : c + n] = folded(b, 1 - place_in, q).astype(BF16)
        step_copy(0 if b == 0 else 2, q).start()

    def fold_step(q):
        c, n = cuts[q]
        step_copy(0, q).wait_recv()
        total = folded(0, place_in, q) + step_in[0, :, c : c + n].astype(F32)
        step_out[1, :, c : c + n] = total.astype(BF16)
        step_copy(1, q).start()

    own.wait_recv()
    for s in range(1, n_z):
        complete(s)
    gate_tiles = gate_cols // 256
    lax.fori_loop(0, gate_tiles, functools.partial(gate_tile, 0), 0)
    far_weight = weights_of(0)
    multiply(0, 0, 0, far_weight)
    multiply(0, 0, 1, far_weight)
    fold_pair(0, 0, 0)
    multiply(0, 1, 0, far_weight)
    fold_pair(0, 0, 1)
    multiply(0, 1, 1, far_weight)
    fold_pair(0, 1, 0)
    lax.fori_loop(0, gate_tiles // 2, functools.partial(gate_tile, 1), 0)
    fold_pair(0, 1, 1)
    fold_side(0, 0)
    lax.fori_loop(gate_tiles // 2, gate_tiles, functools.partial(gate_tile, 1), 0)
    near_weight = weights_of(1)
    multiply(1, 0, 0, near_weight)
    fold_side(0, 1)
    multiply(1, 0, 1, near_weight)
    fold_pair(1, 0, 0)
    fold_step(0)
    multiply(1, 1, 0, near_weight)
    fold_pair(1, 0, 1)
    fold_step(1)
    multiply(1, 1, 1, near_weight)
    fold_pair(1, 1, 0)
    fold_pair(1, 1, 1)
    for q in range(2):
        fold_side(1, q)
    for q, (c, n) in enumerate(cuts):
        total = own_part[:, c : c + n] + folded(1, place_in, q)
        step_copy(1, q).wait_recv()
        total = total + step_in[1, :, c : c + n].astype(F32)
        step_copy(2, q).wait_recv()
        total = total + step_in[2, :, c : c + n].astype(F32)
        own_part[:, c : c + n] = total
    for c, n in half_blocks:
        picked = tail_order if n == tail_size else order
        out[:, c : c + n] = matmul(own_part[:, c : c + n].astype(BF16), picked, (1, 1)).astype(BF16)

    own.wait_send()
    for side in range(2):

        @pl.when(goes(side))
        def _():
            for k in range(CHUNKS):
                line_copy(side, 1, k, z).wait_send()

    for s in range(1, n_z):
        drain(s)
    for q in range(2):
        for b in range(2):
            for h in range(2):
                pair_copy(b, h, q).wait_send()
            side_copy(b, q).wait_send()
        for i in range(3):
            step_copy(i, q).wait_send()


def dense_shards(
    hidden,
    route_experts,
    route_weight,
    norm_gain,
    gate_up_codes,
    gate_up_scales,
    gate_up_bias,
    down_codes,
    down_scales,
    down_bias,
):
    ep_count = lax.axis_size("ep")
    tok, width = hidden.shape
    n_z = ep_count // 2
    half = width // 2
    units = down_codes.shape[1]
    first_cut = -(-half // 256) * 128
    cuts = ((0, first_cut), (first_cut, half - first_cut))
    dma = pltpu.SemaphoreType.DMA
    vmem = pltpu.VMEM
    in_vmem, anywhere = pl.BlockSpec(memory_space=vmem), pl.BlockSpec(memory_space=pl.ANY)
    return pl.pallas_call(
        functools.partial(layer_kernel, (tok, width, n_z, cuts)),
        out_shape=jax.ShapeDtypeStruct((tok, half), BF16),
        in_specs=[in_vmem] * 4 + [anywhere] + [in_vmem] * 2 + [anywhere] + [in_vmem] * 2,
        out_specs=in_vmem,
        scratch_shapes=[
            vmem(gate_up_codes.shape[1:], jnp.int32),
            vmem((down_codes.shape[2], units), jnp.int32),
            vmem((half // 64 * 8, units), jnp.int32),
            vmem(gate_up_scales.shape[1:], F32),
            vmem((2, half, 128), BF16),
            vmem((tok, half), F32),
            vmem((1, half), F32),
            vmem((ep_count * tok, width + SPARE), BF16),
            vmem((width + SPARE, gate_up_codes.shape[2]), BF16),
            vmem((2, half, units), BF16),
            vmem((2, ep_count * tok // 2, units), BF16),
            vmem((2, 2, 2, tok, half), BF16),
            vmem((2, 2, 2, tok, half), BF16),
            vmem((2, 2, tok, half), BF16),
            vmem((2, 2, tok, half), BF16),
            vmem((2, 2, 2, tok, half), BF16),
            vmem((3, tok, half), BF16),
            vmem((3, tok, half), BF16),
            dma((2,)),
            dma,
            dma,
            dma((2, n_z, CHUNKS)),
            dma((2, n_z, CHUNKS)),
            dma((2, n_z, CHUNKS)),
            dma((2, n_z, CHUNKS)),
            dma((2, n_z, CHUNKS, 2)),
            dma((2, n_z, CHUNKS, 2)),
            dma((2, 2, 2)),
            dma((2, 2, 2)),
            dma((2, 2)),
            dma((2, 2)),
            dma((3, 2)),
            dma((3, 2)),
        ],
        compiler_params=pltpu.CompilerParams(
            collective_id=0, has_side_effects=True, vmem_limit_bytes=63 * 1024 * 1024
        ),
    )(
        hidden,
        route_experts.T,
        route_weight.T,
        norm_gain.reshape(1, width),
        gate_up_codes[0],
        gate_up_scales[0],
        gate_up_bias,
        down_codes[0].T,
        down_scales[0],
        down_bias,
    )


def solution(mesh):
    def layer(*arrays):
        tok, top = arrays[1].shape
        ep_count, tp_count = lax.axis_size("ep"), lax.axis_size("tp")
        dense = 2 * top >= ep_count and tp_count == 2 and ep_count == 8 and tok == 64
        return (dense_shards if dense else shards)(*arrays)

    placed = (
        P(("groups", "ep"), None),
        P(("groups", "ep"), None),
        P(("groups", "ep"), None),
        P(),
        P("ep", None, "tp"),
        P("ep", None, "tp"),
        P("ep", "tp"),
        P("ep", "tp", None),
        P("ep", "tp", None),
        P("ep", "tp"),
    )
    return jax.shard_map(
        layer, mesh=mesh, in_specs=placed, out_specs=P(("groups", "ep"), "tp"), check_vma=False
    )
```

time: 86.9 us -> 74.5 us (0.86)
  Pallas kernels: 78.2 us -> 71.4 us
  local copies, waits for them, and re-layouts: 8.51 us -> 2.91 us
    pallas_call x1, Pallas kernels: 78.2 us -> 71.4 us  [dense_shards(): pl.pallas_call(functools.partial(layer_kernel, (tok, width, n_z, cuts)),...]
    unnamed x4 -> x1, local copies, waits for them, and re-layouts: 7.21 us -> 1.62 us
where the time goes in v1:
time: 74.5 us; the launch traced here: 74.3 us
  Pallas kernels  71.4 us (96%)
  local copies, waits for them, and re-layouts  2.91 us (4%)
    pallas_call x1, Pallas kernels, dense_shards(): pl.pallas_call(functools.partial(layer_kernel, (tok, width, n_z, cuts)),...  71.4 us
    unnamed x1, local copies, waits for them, and re-layouts  1.62 us

profile of v1, /device:TPU:0, one launch (start us, length us, event | category | flops | bytes accessed | tf_op | source)
XLA Modules:
  0.0 74.3 jit_solution(12181407556925808453)
XLA Ops:
  0.0 1.3 %reshape.3.gain = bf16[1,2880]{1,0:T(2,128)(2,1)} reshape(bf16[2880]{0:T(1024)(128)(2,1)} %param.13) | data formatting | bytes 11520 | tf_op jit(solution)/shard_map/reshape | solution.py:710
  1.3 71.4 %shard_map.100 = bf16[64,1440]{1,0:T(8,128)(2,1)} custom-call(bf16[64,2880]{1,0:T(8,128)(2,1)} %hidden.1, s32[4,64]{1,0:T(4,128)} %bitcast.12, f32[4,64]{1,0:T(4,128)} %bitcast.13, bf16[1,2880]{1,0:T(2,128)(2,1)} %reshape.3.gain, s32[360,2560]{1,0:T(8,128)} %bitcast.8, bf16[90,2560]{1,0:T(8,128)(2,1)} %bitcast.10, bf16[1,2560]{1,0:T(2,128)(2,1)} %gate_bias.1, ...), custom_call_target="tpu_custom_call" | custom-call | tf_op jit(solution)/shard_map/pallas_call | solution.py:663
  72.7 1.6 %copy.12 = bf16[64,1440]{1,0:T(8,128)(2,1)} copy(bf16[64,1440]{1,0:T(8,128)(2,1)} %shard_map.100) | data formatting | bytes 368640

commit v2 on v1

--- a/solution.py
+++ b/solution.py
@@ -139,18 +139,26 @@
     return blocks + ([(total // 256 * 256, total % 256)] if total % 256 else [])
 
 
-def decoded(words, quad, negative, scale):
-    doubled = lax.shift_right_logical(jnp.full_like(words, MAGNITUDES), quad) & 15
-    return doubled.astype(F32) * jnp.where(negative, -scale, scale)
+def magnitude(words, quad):
+    return (lax.shift_right_logical(jnp.full_like(words, MAGNITUDES), quad) & 15).astype(F32)
 
 
 def decode_words(words, scales):
     pieces = []
-    for j in range(8):
-        moved = jnp.left_shift(words, 2) if j == 0 else lax.shift_right_logical(words, 4 * j - 2)
-        negative = (words if j == 7 else jnp.left_shift(words, 28 - 4 * j)) < 0
-        pieces.append(decoded(words, moved & 28, negative, scales[j]))
-    return jnp.concatenate(pieces, axis=0).astype(BF16)
+    for quarter in range(4):
+        j = 2 * quarter
+        upper = words if j < 4 else lax.shift_right_logical(words, 16)
+        pair = jnp.concatenate([upper, lax.shift_right_logical(words, 4 + j // 4 * 16)], axis=0)
+        negative = (pair.astype(jnp.int16) & jnp.int16(8 << (4 * (j % 4)))) != 0
+        sizes = []
+        for i in (j, j + 1):
+            moved = jnp.left_shift(words, 2) if i == 0 else lax.shift_right_logical(words, 4 * i - 2)
+            sizes.append(magnitude(words, moved & 28))
+        scale = scales[quarter]
+        pieces.append(
+            jnp.concatenate(sizes, axis=0).astype(BF16) * jnp.where(negative, -scale, scale)
+        )
+    return jnp.concatenate(pieces, axis=0)
 
 
 def layer_kernel(
@@ -214,7 +222,6 @@
     beyond = (z + 2) % 4
     neighbour = {"ep": 2 * beside + core}
     opposite = {"ep": 2 * beyond + core}
-    along = [{"ep": 2 * ((z + 1) % n_z) + core}, {"ep": 2 * ((z + n_z - 1) % n_z) + core}]
 
     def copy(src, dst, send, recv, device):
         return pltpu.make_async_remote_copy(
@@ -279,97 +286,103 @@
         start = (2 * chip + core) * tok + half * half_rows + k * part_rows
         return rows_in.at[pl.ds(pl.multiple_of(start, part_rows), part_rows)]
 
+    near = 1 - z % 2
+
+    def origin(side, s):
+        return (z + n_z + (2 * side - 1) * s) % n_z
+
+    def has(side, s):
+        return side * (n_z - 1 - z) + (1 - side) * z >= s
+
+    def goes(side):
+        return side * z + (1 - side) * (n_z - 1 - z) >= 1
+
     def line_copy(side, s, k, chip):
-        return copy(
-            part(chip, x, k),
-            part(chip, x, k),
-            line_send.at[side, s, k],
-            line_recv.at[side, s, k],
-            along[side],
-        )
-
-    def origin(side, s):
-        return (z + n_z - s) % n_z if side == 0 else (z + s) % n_z
-
-    def has(side, s):
-        return z >= s if side == 0 else z + s < n_z
-
-    def goes(side):
-        return z < n_z - 1 if side == 0 else z > 0
-
-    def both(side, s):
-        return (z >= s) & (z < n_z - 1) if side == 0 else (z + s < n_z) & (z > 0)
+        ref = part(chip, x, k)
+        onward = {"ep": 2 * ((z + n_z + 1 - 2 * side) % n_z) + core}
+        return copy(ref, ref, line_send.at[side, s, k], line_recv.at[side, s, k], onward)
+
+    def cross_copy(side, s, k):
+        ref = part(origin(side, s), x, k)
+        return copy(ref, ref, cross_send.at[side, s, k], cross_recv.at[side, s, k], across)
+
+    def pass_copy(side, s, k, i):
+        ref = part(origin(side, s), x if i == 0 else 1 - x, k)
+        return copy(ref, ref, pass_send.at[side, s, k, i], pass_recv.at[side, s, k, i], partner)
+
+    def when(condition, action):
+        pl.when(condition)(action)
 
     for k in range(CHUNKS):
         for side in range(2):
-
-            @pl.when(goes(side))
-            def _():
-                line_copy(side, 1, k, z).start()
+            when(goes(side), lambda: line_copy(side, 1, k, z).start())
 
     own_block = rows_in.at[mine]
     own = copy(own_block, own_block, own_send, own_recv, partner)
     own.start()
 
-    def cross_copy(side, s, k):
-        ref = part(origin(side, s), x, k)
-        return copy(ref, ref, cross_send.at[side, s, k], cross_recv.at[side, s, k], across)
-
-    def pass_copy(side, s, k, i):
-        ref = part(origin(side, s), x if i == 0 else 1 - x, k)
-        return copy(ref, ref, pass_send.at[side, s, k, i], pass_recv.at[side, s, k, i], partner)
-
-    def arrive(s, k):
-        for side in range(2):
-
-            @pl.when(has(side, s))
-            def _():
-                line_copy(side, s, k, origin(side, s)).wait_recv()
+    def arrive(side, s, k):
+        def action():
+            line_copy(side, s, k, origin(side, s)).wait_recv()
+            if s < n_z - 1:
+                when(goes(side), lambda: line_copy(side, s + 1, k, origin(side, s)).start())
+            pass_copy(side, s, k, 0).start()
+
+        when(has(side, s), action)
+
+    def cross(side, s, k):
+        when(has(side, s), lambda: cross_copy(side, s, k).start())
+
+    def arrive_crossed(side, s, k):
+        def action():
+            cross_copy(side, s, k).wait_recv()
+            pass_copy(side, s, k, 1).start()
+
+        when(has(side, s), action)
+
+    def complete(side, s):
+        def action():
+            for k in range(CHUNKS):
+                for i in range(2):
+                    pass_copy(side, s, k, i).wait_recv()
+
+        when(has(side, s), action)
+
+    def drain(side, s):
+        def action():
+            for k in range(CHUNKS):
+                cross_copy(side, s, k).wait_send()
+                for i in range(2):
+                    pass_copy(side, s, k, i).wait_send()
                 if s < n_z - 1:
-
-                    @pl.when(goes(side))
-                    def _():
-                        line_copy(side, s + 1, k, origin(side, s)).start()
-
-                cross_copy(side, s, k).start()
-                pass_copy(side, s, k, 0).start()
-
-    def arrive_crossed(s, k):
-        for side in range(2):
-
-            @pl.when(has(side, s))
-            def _():
-                cross_copy(side, s, k).wait_recv()
-                pass_copy(side, s, k, 1).start()
-
-    def complete(s):
-        for side in range(2):
-
-            @pl.when(has(side, s))
-            def _():
-                for k in range(CHUNKS):
-                    for i in range(2):
-                        pass_copy(side, s, k, i).wait_recv()
-
-    def drain(s):
-        for side in range(2):
-
-            @pl.when(has(side, s))
-            def _():
-                for k in range(CHUNKS):
-                    cross_copy(side, s, k).wait_send()
-                    for i in range(2):
-                        pass_copy(side, s, k, i).wait_send()
-                    if s < n_z - 1:
-
-                        @pl.when(goes(side))
-                        def _():
-                            line_copy(side, s + 1, k, origin(side, s)).wait_send()
+                    when(
+                        goes(side),
+                        lambda: line_copy(side, s + 1, k, origin(side, s)).wait_send(),
+                    )
+
+        when(has(side, s), action)
+
+    far = 1 - near
+
+    def first_arrives(k):
+        arrive(near, 1, k)
+        arrive(far, 1, k)
+        cross(near, 1, k)
+
+    def later_arrives(s, k):
+        arrive(near, s, k)
+        arrive(far, s, k)
+        cross(near, s, k)
+        cross(far, s, k)
+
+    def crossed(s, k):
+        arrive_crossed(near, s, k)
+        arrive_crossed(far, s, k)
 
     gate_scales[...] = gate_scales_in[...].astype(F32) * 0.5
     gate_cols = gate_codes.shape[1]
     col_step = 512 if gate_cols % 512 == 0 else 256
-    upper = lax.broadcasted_iota(jnp.int32, (8, col_step), 0) < 4
+    upper = lax.broadcasted_iota(jnp.int32, (16, col_step), 0) % 8 < 4
 
     def gate_rows(s, carry):
         base = pl.multiple_of(s * 8, 8)
@@ -377,29 +390,29 @@
             words = gate_codes[pl.ds(base, 8), col : col + col_step]
             first, second = (
                 jnp.broadcast_to(
-                    gate_scales[pl.ds(2 * s + i, 1), col : col + col_step], (8, col_step)
+                    gate_scales[pl.ds(2 * s + i, 1), col : col + col_step], (16, col_step)
                 )
                 for i in range(2)
             )
-            scale = jnp.where(upper, first, second)
+            scale = jnp.where(upper, first, second).astype(BF16)
             gate_weight[pl.ds(pl.multiple_of(s * 64, 64), 64), col : col + col_step] = (
-                decode_words(words, [scale] * 8)
+                decode_words(words, [scale] * 4)
             )
         return carry
 
     gate_steps = gate_codes.shape[0] // 8
     gate_weight[pl.ds(width, SPARE), :] = jnp.zeros((SPARE, gate_cols), BF16)
     loads[0].wait()
-    marks = [0, 12, 23, 34, gate_steps]
-    services = [
-        lambda: arrive(1, 0),
-        lambda: arrive(1, 1),
-        lambda: (arrive(2, 0), arrive_crossed(1, 0)),
-        lambda: (arrive(2, 1), arrive_crossed(1, 1)),
-    ]
-    for low_mark, high_mark, service in zip(marks[:-1], marks[1:], services):
-        lax.fori_loop(low_mark, high_mark, gate_rows, 0)
-        service()
+    marks = [0, gate_steps * 24 // 45, gate_steps * 35 // 45, gate_steps]
+    lax.fori_loop(marks[0], marks[1], gate_rows, 0)
+    first_arrives(0)
+    lax.fori_loop(marks[1], marks[2], gate_rows, 0)
+    first_arrives(1)
+    for k in range(CHUNKS):
+        cross(far, 1, k)
+    lax.fori_loop(marks[2], marks[3], gate_rows, 0)
+    later_arrives(2, 0)
+    arrive_crossed(near, 1, 0)
 
     scale_rows = down_scales_in.shape[0]
     half_blocks = column_blocks(half_cols)
@@ -428,16 +441,17 @@
     shifted_codes[...] = down_codes[words_half : words_half + down_steps * 8, :]
 
     def down_rows(h, g, carry):
-        base = pl.multiple_of(g * 64, 64)
+        base = pl.multiple_of(g * 128, 128)
         source = down_codes if h == 0 else shifted_codes
-        start = pl.multiple_of(g * 8, 8)
-        scale_block = down_scales[h, pl.ds(base, 64), :scale_rows]
+        scale_block = down_scales[h, pl.ds(base, 128), :scale_rows]
         for col in range(0, units, 256):
-            scale = matmul(scale_block, spread[:, col : col + 256])
-            words = source[pl.ds(start, 8), col : col + 256]
-            down_weight[h, pl.ds(base, 64), col : col + 256] = decode_words(
-                words, [scale[8 * j : 8 * j + 8] for j in range(8)]
-            )
+            scale = matmul(scale_block, spread[:, col : col + 256]).astype(BF16)
+            for i in range(2):
+                words = source[pl.ds(pl.multiple_of(g * 16 + 8 * i, 8), 8), col : col + 256]
+                start = pl.multiple_of(base + 64 * i, 64)
+                down_weight[h, pl.ds(start, 64), col : col + 256] = decode_words(
+                    words, [scale[64 * i + 16 * j : 64 * i + 16 * j + 16] for j in range(4)]
+                )
         return carry
 
     place = (lax.broadcasted_iota(jnp.int32, (8, units), 0) >> 2) * 4
@@ -452,56 +466,56 @@
             shift = place + 8 * i
             quad = jnp.left_shift(lax.shift_right_logical(words, shift), 2) & 28
             negative = jnp.left_shift(words, 28 - shift) < 0
-            pieces.append(decoded(words, quad, negative, scale[8 * i : 8 * i + 8]))
+            part_scale = scale[8 * i : 8 * i + 8]
+            pieces.append(magnitude(words, quad) * jnp.where(negative, -part_scale, part_scale))
         down_weight[h, base : base + 32, :] = jnp.concatenate(pieces, axis=0).astype(BF16)
 
-    middle_step = down_steps // 2
+    pair_steps = down_steps // 2
+    middle_step = pair_steps // 2
     lax.fori_loop(0, middle_step, functools.partial(down_rows, 0), 0)
-    arrive(3, 0)
-    lax.fori_loop(middle_step, down_steps, functools.partial(down_rows, 0), 0)
-    arrive_crossed(2, 0)
-    arrive(3, 1)
+    later_arrives(2, 1)
+    arrive_crossed(near, 1, 1)
+    lax.fori_loop(middle_step, pair_steps, functools.partial(down_rows, 0), 0)
+    arrive_crossed(far, 1, 0)
     lax.fori_loop(0, middle_step, functools.partial(down_rows, 1), 0)
-    arrive_crossed(2, 1)
-    lax.fori_loop(middle_step, down_steps, functools.partial(down_rows, 1), 0)
+    later_arrives(3, 0)
+    lax.fori_loop(middle_step, pair_steps, functools.partial(down_rows, 1), 0)
+    arrive_crossed(far, 1, 1)
+    crossed(2, 0)
     down_last(0)
     down_last(1)
-    arrive_crossed(3, 0)
-    arrive_crossed(3, 1)
 
     picks = (
         lax.broadcasted_iota(jnp.int32, (256, 128), 0)
         == 2 * lax.broadcasted_iota(jnp.int32, (256, 128), 1)
     ).astype(F32).astype(BF16)
     batch_rows = 4 * tok
-    near = z // 2
+    group = z // 2
     place_in = z % 2
-    starts = [pl.multiple_of((1 - near) * batch_rows, batch_rows),
-              pl.multiple_of(near * batch_rows, batch_rows)]
-
-    def gate_tile(b, t, carry):
-        cols = pl.ds(pl.multiple_of(t * 256, 256), 256)
+    starts = [
+        pl.multiple_of(group * batch_rows, batch_rows),
+        pl.multiple_of((1 - group) * batch_rows, batch_rows),
+    ]
+    tile_cols = gate_cols // 2
+
+    def gate_tile(b, t):
         projected = jnp.dot(
             rows_in[pl.ds(starts[b], batch_rows), :],
-            gate_weight[:, cols],
+            gate_weight[:, t * tile_cols : (t + 1) * tile_cols],
             preferred_element_type=F32,
-        ) + gate_bias[:, cols].astype(F32)
+        ) + gate_bias[:, t * tile_cols : (t + 1) * tile_cols].astype(F32)
         gate_part = jnp.minimum(projected, 7.0)
-        upward = pltpu.roll(jnp.clip(projected, -7.0, 7.0), 255, 1)
-        value = gate_part * jax.nn.sigmoid(1.702 * gate_part) * (upward + 1.0)
-        activated[b, :, pl.ds(pl.multiple_of(t * 128, 128), 128)] = jnp.dot(
-            value.astype(BF16), picks, preferred_element_type=F32
-        ).astype(BF16)
-        return carry
-
-    def sections(ref, b, h, q):
-        c, n = cuts[q]
-        return ref.at[b, h, :, :, pl.ds(c, n)]
+        upward = pltpu.roll(jnp.clip(projected, -7.0, 7.0), tile_cols - 1, 1)
+        value = (gate_part * jax.nn.sigmoid(1.702 * gate_part) * (upward + 1.0)).astype(BF16)
+        for c in range(0, tile_cols, 256):
+            at = (t * tile_cols + c) // 2
+            activated[b, :, at : at + 128] = matmul(value[:, c : c + 256], picks).astype(BF16)
 
     def pair_copy(b, h, q):
+        c, n = cuts[q]
         return copy(
-            sections(pair_out, b, h, q),
-            sections(pair_in, b, h, q),
+            pair_out.at[b, h, :, :, pl.ds(c, n)],
+            pair_in.at[b, h, :, :, pl.ds(c, n)],
             pair_send.at[b, h, q],
             pair_recv.at[b, h, q],
             partner,
@@ -524,7 +538,7 @@
             step_in.at[i, :, pl.ds(c, n)],
             step_send.at[i, q],
             step_recv.at[i, q],
-            opposite if i == 1 else neighbour,
+            opposite if i == 2 else neighbour,
         )
 
     tail = lax.broadcasted_iota(jnp.int32, (batch_rows, SPARE), 1)
@@ -534,19 +548,21 @@
         hit = (tail == ep) | (tail == ep + 2 * n_z) | (tail == ep + 4 * n_z)
         return jnp.sum(jnp.where(hit, extra, 0.0), axis=1, keepdims=True)
 
-    def multiply(b, h, q, weight):
-        c, n = cuts[q]
+    parts = range(len(cuts))
+
+    def multiply(b, h, weight):
         which = 1 - x if h == 0 else x
-        value = matmul(activated[b], down_weight[which, c : c + n, :], (1, 1))
+        value = matmul(activated[b], down_weight[which], (1, 1))
         if h == 1:
-            value = value + bias_part[:, c : c + n]
+            value = value + bias_part[...]
         value = value * weight
         for i in range(2):
             first = value[2 * i * tok : (2 * i + 1) * tok]
             second = value[(2 * i + 1) * tok : (2 * i + 2) * tok]
-            pair_out[b, h, i, :, c : c + n] = jnp.where(core == 0, second, first).astype(BF16)
-            kept[b, h, i, :, c : c + n] = jnp.where(core == 0, first, second).astype(BF16)
-        pair_copy(b, h, q).start()
+            pair_out[b, h, i] = jnp.where(core == 0, second, first).astype(BF16)
+            kept[b, h, i] = jnp.where(core == 0, first, second).astype(BF16)
+        for q in parts:
+            pair_copy(b, h, q).start()
 
     def fold_pair(b, h, q):
         c, n = cuts[q]
@@ -567,69 +583,90 @@
     def fold_side(b, q):
         c, n = cuts[q]
         side_copy(b, q).wait_recv()
-        step_out[0 if b == 0 else 2, :, c : c + n] = folded(b, 1 - place_in, q).astype(BF16)
-        step_copy(0 if b == 0 else 2, q).start()
+        step_out[b, :, c : c + n] = folded(b, 1 - place_in, q).astype(BF16)
+        step_copy(b, q).start()
+        if b == 0:
+            own_part[:, c : c + n] = own_part[:, c : c + n] + folded(0, place_in, q)
 
     def fold_step(q):
         c, n = cuts[q]
-        step_copy(0, q).wait_recv()
-        total = folded(0, place_in, q) + step_in[0, :, c : c + n].astype(F32)
-        step_out[1, :, c : c + n] = total.astype(BF16)
-        step_copy(1, q).start()
+        step_copy(1, q).wait_recv()
+        total = folded(1, place_in, q) + step_in[1, :, c : c + n].astype(F32)
+        step_out[2, :, c : c + n] = total.astype(BF16)
+        step_copy(2, q).start()
+
+    def add_step(i, q):
+        c, n = cuts[q]
+        step_copy(i, q).wait_recv()
+        own_part[:, c : c + n] = own_part[:, c : c + n] + step_in[i, :, c : c + n].astype(F32)
+
+    def write_out(q):
+        c, n = cuts[q]
+        at = c
+        while at < c + n:
+            left = half_cols - at
+            size = tail_size if left == tail_size else min(256, c + n - at)
+            if left > tail_size and left - size < tail_size:
+                size = left - tail_size
+            picked = tail_order if left == tail_size else order[:size, :size]
+            block = own_part[:, at : at + size].astype(BF16)
+            out[:, at : at + size] = matmul(block, picked, (1, 1)).astype(BF16)
+            at += size
 
     own.wait_recv()
-    for s in range(1, n_z):
-        complete(s)
-    gate_tiles = gate_cols // 256
-    lax.fori_loop(0, gate_tiles, functools.partial(gate_tile, 0), 0)
-    far_weight = weights_of(0)
-    multiply(0, 0, 0, far_weight)
-    multiply(0, 0, 1, far_weight)
-    fold_pair(0, 0, 0)
-    multiply(0, 1, 0, far_weight)
-    fold_pair(0, 0, 1)
-    multiply(0, 1, 1, far_weight)
-    fold_pair(0, 1, 0)
-    lax.fori_loop(0, gate_tiles // 2, functools.partial(gate_tile, 1), 0)
-    fold_pair(0, 1, 1)
-    fold_side(0, 0)
-    lax.fori_loop(gate_tiles // 2, gate_tiles, functools.partial(gate_tile, 1), 0)
-    near_weight = weights_of(1)
-    multiply(1, 0, 0, near_weight)
-    fold_side(0, 1)
-    multiply(1, 0, 1, near_weight)
-    fold_pair(1, 0, 0)
-    fold_step(0)
-    multiply(1, 1, 0, near_weight)
-    fold_pair(1, 0, 1)
-    fold_step(1)
-    multiply(1, 1, 1, near_weight)
-    fold_pair(1, 1, 0)
-    fold_pair(1, 1, 1)
-    for q in range(2):
+    complete(near, 1)
+    near_weight = weights_of(0)
+    gate_tile(0, 0)
+    later_arrives(3, 1)
+    crossed(2, 1)
+    gate_tile(0, 1)
+    crossed(3, 0)
+    multiply(0, 0, near_weight)
+    crossed(3, 1)
+    multiply(0, 1, near_weight)
+    for q in parts:
+        fold_pair(0, 0, q)
+    for q in parts:
+        fold_pair(0, 1, q)
+    complete(far, 1)
+    for s in range(2, n_z):
+        complete(0, s)
+        complete(1, s)
+    far_weight = weights_of(1)
+    gate_tile(1, 0)
+    for q in (0, 1):
+        fold_side(0, q)
+    gate_tile(1, 1)
+    multiply(1, 0, far_weight)
+    fold_side(0, 2)
+    for q in parts:
+        fold_pair(1, 0, q)
+    multiply(1, 1, far_weight)
+    fold_side(0, 3)
+    for q in parts:
+        fold_pair(1, 1, q)
+    for q in parts:
+        add_step(0, q)
+    for q in parts:
         fold_side(1, q)
-    for q, (c, n) in enumerate(cuts):
-        total = own_part[:, c : c + n] + folded(1, place_in, q)
-        step_copy(1, q).wait_recv()
-        total = total + step_in[1, :, c : c + n].astype(F32)
-        step_copy(2, q).wait_recv()
-        total = total + step_in[2, :, c : c + n].astype(F32)
-        own_part[:, c : c + n] = total
-    for c, n in half_blocks:
-        picked = tail_order if n == tail_size else order
-        out[:, c : c + n] = matmul(own_part[:, c : c + n].astype(BF16), picked, (1, 1)).astype(BF16)
+        if q:
+            fold_step(q - 1)
+    fold_step(len(cuts) - 1)
+    for q in parts:
+        add_step(2, q)
+        write_out(q)
 
     own.wait_send()
     for side in range(2):
 
-        @pl.when(goes(side))
-        def _():
+        def sent():
             for k in range(CHUNKS):
                 line_copy(side, 1, k, z).wait_send()
 
-    for s in range(1, n_z):
-        drain(s)
-    for q in range(2):
+        when(goes(side), sent)
+        for s in range(1, n_z):
+            drain(side, s)
+    for q in parts:
         for b in range(2):
             for h in range(2):
                 pair_copy(b, h, q).wait_send()
@@ -655,8 +692,8 @@
     n_z = ep_count // 2
     half = width // 2
     units = down_codes.shape[1]
-    first_cut = -(-half // 256) * 128
-    cuts = ((0, first_cut), (first_cut, half - first_cut))
+    step = -(-half // 512) * 128
+    cuts = tuple((c, min(step, half - c)) for c in range(0, half, step))
     dma = pltpu.SemaphoreType.DMA
     vmem = pltpu.VMEM
     in_vmem, anywhere = pl.BlockSpec(memory_space=vmem), pl.BlockSpec(memory_space=pl.ANY)
@@ -693,12 +730,12 @@
             dma((2, n_z, CHUNKS)),
             dma((2, n_z, CHUNKS, 2)),
             dma((2, n_z, CHUNKS, 2)),
-            dma((2, 2, 2)),
-            dma((2, 2, 2)),
-            dma((2, 2)),
-            dma((2, 2)),
-            dma((3, 2)),
-            dma((3, 2)),
+            dma((2, 2, 4)),
+            dma((2, 2, 4)),
+            dma((2, 4)),
+            dma((2, 4)),
+            dma((3, 4)),
+            dma((3, 4)),
         ],
         compiler_params=pltpu.CompilerParams(
             collective_id=0, has_side_effects=True, vmem_limit_bytes=63 * 1024 * 1024

time: 74.5 us -> 67.3 us (0.903)
  Pallas kernels: 71.4 us -> 64.1 us
    pallas_call x1, Pallas kernels: 71.4 us -> 64.1 us  [dense_shards(): pl.pallas_call(functools.partial(layer_kernel, (tok, width, n_z, cuts)),...]
where the time goes in v2:
time: 67.3 us; the launch traced here: 67.1 us
  Pallas kernels  64.1 us (95%)
  local copies, waits for them, and re-layouts  2.91 us (4%)
    pallas_call x1, Pallas kernels, dense_shards(): pl.pallas_call(functools.partial(layer_kernel, (tok, width, n_z, cuts)),...  64.1 us
    unnamed x1, local copies, waits for them, and re-layouts  1.62 us

profile of v2, /device:TPU:0, one launch (start us, length us, event | category | flops | bytes accessed | tf_op | source)
XLA Modules:
  0.0 67.1 jit_solution(614903255276987440)
XLA Ops:
  0.0 1.3 %reshape.3.gain = bf16[1,2880]{1,0:T(2,128)(2,1)} reshape(bf16[2880]{0:T(1024)(128)(2,1)} %param.13) | data formatting | bytes 11520 | tf_op jit(solution)/shard_map/reshape | solution.py:747
  1.3 64.1 %shard_map.100 = bf16[64,1440]{1,0:T(8,128)(2,1)} custom-call(bf16[64,2880]{1,0:T(8,128)(2,1)} %hidden.1, s32[4,64]{1,0:T(4,128)} %bitcast.12, f32[4,64]{1,0:T(4,128)} %bitcast.13, bf16[1,2880]{1,0:T(2,128)(2,1)} %reshape.3.gain, s32[360,2560]{1,0:T(8,128)} %bitcast.8, bf16[90,2560]{1,0:T(8,128)(2,1)} %bitcast.10, bf16[1,2560]{1,0:T(2,128)(2,1)} %gate_bias.1, ...), custom_call_target="tpu_custom_call" | custom-call | tf_op jit(solution)/shard_map/pallas_call | solution.py:700
  65.5 1.6 %copy.12 = bf16[64,1440]{1,0:T(8,128)(2,1)} copy(bf16[64,1440]{1,0:T(8,128)(2,1)} %shard_map.100) | data formatting | bytes 368640

commit v3 on v2

--- a/solution.py
+++ b/solution.py
@@ -176,7 +176,7 @@
     out,
     gate_codes,
     down_codes,
-    shifted_codes,
+    half_codes,
     gate_scales,
     down_scales,
     own_part,
@@ -237,8 +237,7 @@
         pltpu.make_async_copy(gate_codes_in, gate_codes, load_sem.at[0]),
         pltpu.make_async_copy(down_codes_in, down_codes, load_sem.at[1]),
     ]
-    for load in loads:
-        load.start()
+    loads[0].start()
     barrier = pltpu.get_barrier_semaphore()
     others = [{"ep": 2 * ((z + d) % n_z) + core} for d in range(1, n_z)]
     for device in [partner, across] + others:
@@ -248,11 +247,12 @@
 
     order = word_order(256, False)
     blocks = column_blocks(width)
+    gain_row = gain[...].reshape(1, width)
     wide = jnp.concatenate(
         [matmul(hidden[:, c : c + n], order[:n, :n]) for c, n in blocks], axis=1
     )
     gain_row = jnp.concatenate(
-        [matmul(gain[:, c : c + n], order[:n, :n]) for c, n in blocks], axis=1
+        [matmul(gain_row[:, c : c + n], order[:n, :n]) for c, n in blocks], axis=1
     )
     plain = hidden[...].astype(F32)
     mean_square = jnp.mean(plain * plain, axis=-1, keepdims=True)
@@ -402,18 +402,6 @@
 
     gate_steps = gate_codes.shape[0] // 8
     gate_weight[pl.ds(width, SPARE), :] = jnp.zeros((SPARE, gate_cols), BF16)
-    loads[0].wait()
-    marks = [0, gate_steps * 24 // 45, gate_steps * 35 // 45, gate_steps]
-    lax.fori_loop(marks[0], marks[1], gate_rows, 0)
-    first_arrives(0)
-    lax.fori_loop(marks[1], marks[2], gate_rows, 0)
-    first_arrives(1)
-    for k in range(CHUNKS):
-        cross(far, 1, k)
-    lax.fori_loop(marks[2], marks[3], gate_rows, 0)
-    later_arrives(2, 0)
-    arrive_crossed(near, 1, 0)
-
     scale_rows = down_scales_in.shape[0]
     half_blocks = column_blocks(half_cols)
     tail_size = half_blocks[-1][1]
@@ -429,6 +417,19 @@
         own_part[:, c : c + n] = matmul(shown[:, c : c + n], picked)
         bias_part[:, c : c + n] = matmul(down_bias[:, c : c + n], picked)
 
+    loads[0].wait()
+    loads[1].start()
+    marks = [0, gate_steps * 20 // 45, gate_steps * 30 // 45, gate_steps * 40 // 45]
+    lax.fori_loop(marks[0], marks[1], gate_rows, 0)
+    first_arrives(0)
+    lax.fori_loop(marks[1], marks[2], gate_rows, 0)
+    first_arrives(1)
+    for k in range(CHUNKS):
+        cross(far, 1, k)
+    lax.fori_loop(marks[2], marks[3], gate_rows, 0)
+    later_arrives(2, 0)
+    lax.fori_loop(marks[3], gate_steps, gate_rows, 0)
+
     units = down_codes.shape[1]
     words_half = half_cols // 8
     down_steps = words_half // 8
@@ -438,16 +439,16 @@
     ).astype(F32) * 0.5
     spread = spread.astype(BF16)
     loads[1].wait()
-    shifted_codes[...] = down_codes[words_half : words_half + down_steps * 8, :]
+    for h in range(2):
+        half_codes[h, :words_half] = down_codes[h * words_half : (h + 1) * words_half, :]
 
     def down_rows(h, g, carry):
         base = pl.multiple_of(g * 128, 128)
-        source = down_codes if h == 0 else shifted_codes
         scale_block = down_scales[h, pl.ds(base, 128), :scale_rows]
         for col in range(0, units, 256):
             scale = matmul(scale_block, spread[:, col : col + 256]).astype(BF16)
             for i in range(2):
-                words = source[pl.ds(pl.multiple_of(g * 16 + 8 * i, 8), 8), col : col + 256]
+                words = half_codes[h, pl.ds(pl.multiple_of(g * 16 + 8 * i, 8), 8), col : col + 256]
                 start = pl.multiple_of(base + 64 * i, 64)
                 down_weight[h, pl.ds(start, 64), col : col + 256] = decode_words(
                     words, [scale[64 * i + 16 * j : 64 * i + 16 * j + 16] for j in range(4)]
@@ -458,7 +459,7 @@
 
     def down_last(h):
         base = down_steps * 64
-        four = down_codes[h * words_half + down_steps * 8 : (h + 1) * words_half, :]
+        four = half_codes[h, down_steps * 8 : words_half, :]
         words = jnp.concatenate([four, four], axis=0)
         scale = matmul(down_scales[h, base : base + 32, :scale_rows], spread)
         pieces = []
@@ -472,18 +473,13 @@
 
     pair_steps = down_steps // 2
     middle_step = pair_steps // 2
-    lax.fori_loop(0, middle_step, functools.partial(down_rows, 0), 0)
+    other_rows = functools.partial(down_rows, 1 - x)
     later_arrives(2, 1)
-    arrive_crossed(near, 1, 1)
-    lax.fori_loop(middle_step, pair_steps, functools.partial(down_rows, 0), 0)
-    arrive_crossed(far, 1, 0)
-    lax.fori_loop(0, middle_step, functools.partial(down_rows, 1), 0)
-    later_arrives(3, 0)
-    lax.fori_loop(middle_step, pair_steps, functools.partial(down_rows, 1), 0)
-    arrive_crossed(far, 1, 1)
-    crossed(2, 0)
-    down_last(0)
-    down_last(1)
+    lax.fori_loop(0, middle_step, other_rows, 0)
+    for k in range(CHUNKS):
+        arrive_crossed(near, 1, k)
+    own_ahead = pair_steps // 4
+    lax.fori_loop(0, own_ahead, functools.partial(down_rows, x), 0)
 
     picks = (
         lax.broadcasted_iota(jnp.int32, (256, 128), 0)
@@ -496,20 +492,22 @@
         pl.multiple_of(group * batch_rows, batch_rows),
         pl.multiple_of((1 - group) * batch_rows, batch_rows),
     ]
-    tile_cols = gate_cols // 2
-
-    def gate_tile(b, t):
+
+    def gate_tile(b, t, tile_cols, steps):
+        for step in steps:
+            step()
+        cols = pl.ds(pl.multiple_of(t * tile_cols, tile_cols), tile_cols)
         projected = jnp.dot(
             rows_in[pl.ds(starts[b], batch_rows), :],
-            gate_weight[:, t * tile_cols : (t + 1) * tile_cols],
+            gate_weight[:, cols],
             preferred_element_type=F32,
-        ) + gate_bias[:, t * tile_cols : (t + 1) * tile_cols].astype(F32)
+        ) + gate_bias[:, cols].astype(F32)
         gate_part = jnp.minimum(projected, 7.0)
         upward = pltpu.roll(jnp.clip(projected, -7.0, 7.0), tile_cols - 1, 1)
         value = (gate_part * jax.nn.sigmoid(1.702 * gate_part) * (upward + 1.0)).astype(BF16)
         for c in range(0, tile_cols, 256):
-            at = (t * tile_cols + c) // 2
-            activated[b, :, at : at + 128] = matmul(value[:, c : c + 256], picks).astype(BF16)
+            at = pl.ds(pl.multiple_of(t * (tile_cols // 2) + c // 2, 128), 128)
+            activated[b, :, at] = matmul(value[:, c : c + 256], picks).astype(BF16)
 
     def pair_copy(b, h, q):
         c, n = cuts[q]
@@ -613,46 +611,61 @@
             out[:, at : at + size] = matmul(block, picked, (1, 1)).astype(BF16)
             at += size
 
+    half_tiles = gate_cols // 2
+
+    def decode_steps(which, first, last):
+        steps = [functools.partial(down_rows, which, g, 0) for g in range(first, last)]
+        return steps + ([functools.partial(down_last, which)] if last == pair_steps else [])
+
+    later_arrives(3, 0)
     own.wait_recv()
     complete(near, 1)
     near_weight = weights_of(0)
-    gate_tile(0, 0)
-    later_arrives(3, 1)
-    crossed(2, 1)
-    gate_tile(0, 1)
-    crossed(3, 0)
+    mixed = 512
+    tiles = gate_cols // mixed
+    steps = decode_steps(1 - x, middle_step, pair_steps) + decode_steps(x, own_ahead, pair_steps)
+    services = {
+        0: [lambda: later_arrives(3, 1)],
+        1: [lambda: arrive_crossed(far, 1, 0), lambda: arrive_crossed(far, 1, 1)],
+        2: [lambda: crossed(2, 0)],
+        3: [lambda: crossed(2, 1), lambda: crossed(3, 0)],
+    }
+    for t in range(tiles):
+        cut = len(steps) * t // tiles, len(steps) * (t + 1) // tiles
+        gate_tile(0, t, mixed, steps[cut[0] : cut[1]])
+        for service in services.get(t, []):
+            service()
     multiply(0, 0, near_weight)
     crossed(3, 1)
     multiply(0, 1, near_weight)
     for q in parts:
         fold_pair(0, 0, q)
-    for q in parts:
-        fold_pair(0, 1, q)
     complete(far, 1)
     for s in range(2, n_z):
         complete(0, s)
         complete(1, s)
     far_weight = weights_of(1)
-    gate_tile(1, 0)
-    for q in (0, 1):
-        fold_side(0, q)
-    gate_tile(1, 1)
+    gate_tile(1, 0, half_tiles, [])
+    for q in parts:
+        fold_pair(0, 1, q)
+    gate_tile(1, 1, half_tiles, [])
+    fold_side(0, 0)
+    fold_side(0, 1)
     multiply(1, 0, far_weight)
     fold_side(0, 2)
+    multiply(1, 1, far_weight)
     for q in parts:
         fold_pair(1, 0, q)
-    multiply(1, 1, far_weight)
     fold_side(0, 3)
     for q in parts:
         fold_pair(1, 1, q)
-    for q in parts:
-        add_step(0, q)
     for q in parts:
         fold_side(1, q)
         if q:
             fold_step(q - 1)
     fold_step(len(cuts) - 1)
     for q in parts:
+        add_step(0, q)
         add_step(2, q)
         write_out(q)
 
@@ -692,8 +705,10 @@
     n_z = ep_count // 2
     half = width // 2
     units = down_codes.shape[1]
-    step = -(-half // 512) * 128
-    cuts = tuple((c, min(step, half - c)) for c in range(0, half, step))
+    last = half % 128 + 128
+    step = -(-(half - last) // 384) * 128
+    cuts = tuple((c, min(step, half - last - c)) for c in range(0, half - last, step))
+    cuts += ((half - last, last),)
     dma = pltpu.SemaphoreType.DMA
     vmem = pltpu.VMEM
     in_vmem, anywhere = pl.BlockSpec(memory_space=vmem), pl.BlockSpec(memory_space=pl.ANY)
@@ -705,7 +720,7 @@
         scratch_shapes=[
             vmem(gate_up_codes.shape[1:], jnp.int32),
             vmem((down_codes.shape[2], units), jnp.int32),
-            vmem((half // 64 * 8, units), jnp.int32),
+            vmem((2, -(-half // 64) * 8, units), jnp.int32),
             vmem(gate_up_scales.shape[1:], F32),
             vmem((2, half, 128), BF16),
             vmem((tok, half), F32),
@@ -744,7 +759,7 @@
         hidden,
         route_experts.T,
         route_weight.T,
-        norm_gain.reshape(1, width),
+        norm_gain,
         gate_up_codes[0],
         gate_up_scales[0],
         gate_up_bias,

time: 67.3 us -> 64.4 us (0.957)
  Pallas kernels: 64.1 us -> 62.6 us
  local copies, waits for them, and re-layouts: 2.91 us -> 1.62 us
    pallas_call x1, Pallas kernels: 64.1 us -> 62.6 us  [dense_shards(): pl.pallas_call(functools.partial(layer_kernel, (tok, width, n_z, cuts)),...]
    reshape x1 -> x0, local copies, waits for them, and re-layouts: 1.3 us -> none  [dense_shards(): norm_gain.reshape(1, width)]
where the time goes in v3:
time: 64.4 us; the launch traced here: 64.3 us
  Pallas kernels  62.6 us (97%)
  local copies, waits for them, and re-layouts  1.62 us (3%)
    pallas_call x1, Pallas kernels, dense_shards(): pl.pallas_call(functools.partial(layer_kernel, (tok, width, n_z, cuts)),...  62.6 us
    unnamed x1, local copies, waits for them, and re-layouts  1.62 us

profile of v3, /device:TPU:0, one launch (start us, length us, event | category | flops | bytes accessed | tf_op | source)
XLA Modules:
  0.0 64.3 jit_solution(1529868102433376185)
XLA Ops:
  0.0 62.6 %shard_map.100 = bf16[64,1440]{1,0:T(8,128)(2,1)} custom-call(bf16[64,2880]{1,0:T(8,128)(2,1)} %hidden.1, s32[4,64]{1,0:T(4,128)} %bitcast.12, f32[4,64]{1,0:T(4,128)} %bitcast.13, bf16[2880]{0:T(1024)(128)(2,1)} %gain.1, s32[360,2560]{1,0:T(8,128)} %bitcast.8, bf16[90,2560]{1,0:T(8,128)(2,1)} %bitcast.10, bf16[1,2560]{1,0:T(2,128)(2,1)} %gate_bias.1, ...), custom_call_target="tpu_custom_call" | custom-call | tf_op jit(solution)/shard_map/pallas_call | solution.py:715
  62.6 1.6 %copy.12 = bf16[64,1440]{1,0:T(8,128)(2,1)} copy(bf16[64,1440]{1,0:T(8,128)(2,1)} %shard_map.100) | data formatting | bytes 368640

commit v4 on v3

--- a/solution.py
+++ b/solution.py
@@ -519,13 +519,13 @@
             partner,
         )
 
-    def side_copy(b, q):
+    def side_copy(b, i, q):
         c, n = cuts[q]
         return copy(
-            side_out.at[b, :, :, pl.ds(c, n)],
-            side_in.at[b, :, :, pl.ds(c, n)],
-            side_send.at[b, q],
-            side_recv.at[b, q],
+            side_out.at[b, i, :, pl.ds(c, n)],
+            side_in.at[b, i, :, pl.ds(c, n)],
+            side_send.at[b, i, q],
+            side_recv.at[b, i, q],
             across,
         )
 
@@ -570,33 +570,34 @@
         ].astype(F32)
         if h == 0:
             side_out[b, :, :, c : c + n] = total.astype(BF16)
-            side_copy(b, q).start()
         else:
             kept[b, h, :, :, c : c + n] = total.astype(BF16)
 
     def folded(b, i, q):
         c, n = cuts[q]
+        side_copy(b, i, q).wait_recv()
         return kept[b, 1, i, :, c : c + n].astype(F32) + side_in[b, i, :, c : c + n].astype(F32)
 
     def fold_side(b, q):
         c, n = cuts[q]
-        side_copy(b, q).wait_recv()
         step_out[b, :, c : c + n] = folded(b, 1 - place_in, q).astype(BF16)
         step_copy(b, q).start()
-        if b == 0:
-            own_part[:, c : c + n] = own_part[:, c : c + n] + folded(0, place_in, q)
 
     def fold_step(q):
         c, n = cuts[q]
+        total = folded(1, place_in, q)
         step_copy(1, q).wait_recv()
-        total = folded(1, place_in, q) + step_in[1, :, c : c + n].astype(F32)
+        total = total + step_in[1, :, c : c + n].astype(F32)
         step_out[2, :, c : c + n] = total.astype(BF16)
         step_copy(2, q).start()
 
-    def add_step(i, q):
+    def fold_own(q):
         c, n = cuts[q]
-        step_copy(i, q).wait_recv()
-        own_part[:, c : c + n] = own_part[:, c : c + n] + step_in[i, :, c : c + n].astype(F32)
+        total = own_part[:, c : c + n]
+        for i in (0, 2):
+            step_copy(i, q).wait_recv()
+            total = total + step_in[i, :, c : c + n].astype(F32)
+        own_part[:, c : c + n] = total + folded(0, place_in, q)
 
     def write_out(q):
         c, n = cuts[q]
@@ -611,7 +612,6 @@
             out[:, at : at + size] = matmul(block, picked, (1, 1)).astype(BF16)
             at += size
 
-    half_tiles = gate_cols // 2
 
     def decode_steps(which, first, last):
         steps = [functools.partial(down_rows, which, g, 0) for g in range(first, last)]
@@ -628,45 +628,73 @@
         0: [lambda: later_arrives(3, 1)],
         1: [lambda: arrive_crossed(far, 1, 0), lambda: arrive_crossed(far, 1, 1)],
         2: [lambda: crossed(2, 0)],
-        3: [lambda: crossed(2, 1), lambda: crossed(3, 0)],
+        3: [lambda: crossed(2, 1), lambda: crossed(3, 0), lambda: crossed(3, 1)],
     }
     for t in range(tiles):
         cut = len(steps) * t // tiles, len(steps) * (t + 1) // tiles
         gate_tile(0, t, mixed, steps[cut[0] : cut[1]])
         for service in services.get(t, []):
             service()
-    multiply(0, 0, near_weight)
-    crossed(3, 1)
-    multiply(0, 1, near_weight)
-    for q in parts:
-        fold_pair(0, 0, q)
     complete(far, 1)
     for s in range(2, n_z):
         complete(0, s)
         complete(1, s)
     far_weight = weights_of(1)
-    gate_tile(1, 0, half_tiles, [])
-    for q in parts:
-        fold_pair(0, 1, q)
-    gate_tile(1, 1, half_tiles, [])
-    fold_side(0, 0)
-    fold_side(0, 1)
+    gate_tile(1, 0, gate_cols, [])
     multiply(1, 0, far_weight)
-    fold_side(0, 2)
     multiply(1, 1, far_weight)
+
+    def send(b, which, q):
+        for i in which:
+            side_copy(b, i, q).start()
+
+    def sent(b, which, q):
+        for i in which:
+            side_copy(b, i, q).wait_send()
+
+    theirs, ours = (1 - place_in,), (place_in,)
     for q in parts:
         fold_pair(1, 0, q)
-    fold_side(0, 3)
+        if q < 2:
+            send(1, (0, 1), q)
+    multiply(0, 0, near_weight)
+    multiply(0, 1, near_weight)
+    sent(1, (0, 1), 0)
+    send(1, (0, 1), 2)
     for q in parts:
         fold_pair(1, 1, q)
     for q in parts:
-        fold_side(1, q)
-        if q:
-            fold_step(q - 1)
-    fold_step(len(cuts) - 1)
+        fold_pair(0, 0, q)
     for q in parts:
-        add_step(0, q)
-        add_step(2, q)
+        fold_pair(0, 1, q)
+    fold_side(1, 0)
+    sent(1, (0, 1), 1)
+    send(1, (0, 1), 3)
+    fold_side(1, 1)
+    sent(1, (0, 1), 2)
+    send(0, theirs, 0)
+    send(0, theirs, 1)
+    fold_step(0)
+    fold_side(1, 2)
+    sent(1, (0, 1), 3)
+    send(0, theirs, 2)
+    send(0, theirs, 3)
+    fold_step(1)
+    fold_side(1, 3)
+    for q in (0, 1):
+        sent(0, theirs, q)
+        send(0, ours, q)
+    fold_step(2)
+    for q in (0, 1):
+        fold_side(0, q)
+    for q in (2, 3):
+        sent(0, theirs, q)
+        send(0, ours, q)
+    fold_step(3)
+    for q in (2, 3):
+        fold_side(0, q)
+    for q in parts:
+        fold_own(q)
         write_out(q)
 
     own.wait_send()
@@ -683,7 +711,7 @@
         for b in range(2):
             for h in range(2):
                 pair_copy(b, h, q).wait_send()
-            side_copy(b, q).wait_send()
+        side_copy(0, place_in, q).wait_send()
         for i in range(3):
             step_copy(i, q).wait_send()
 
@@ -705,10 +733,9 @@
     n_z = ep_count // 2
     half = width // 2
     units = down_codes.shape[1]
-    last = half % 128 + 128
-    step = -(-(half - last) // 384) * 128
-    cuts = tuple((c, min(step, half - last - c)) for c in range(0, half - last, step))
-    cuts += ((half - last, last),)
+    step = -(-half // 512) * 128
+    edges = [0] + [step * i - 128 for i in range(1, 4)] + [half]
+    cuts = tuple((low, high - low) for low, high in zip(edges[:-1], edges[1:]))
     dma = pltpu.SemaphoreType.DMA
     vmem = pltpu.VMEM
     in_vmem, anywhere = pl.BlockSpec(memory_space=vmem), pl.BlockSpec(memory_space=pl.ANY)
@@ -747,8 +774,8 @@
             dma((2, n_z, CHUNKS, 2)),
             dma((2, 2, 4)),
             dma((2, 2, 4)),
-            dma((2, 4)),
-            dma((2, 4)),
+            dma((2, 2, 4)),
+            dma((2, 2, 4)),
             dma((3, 4)),
             dma((3, 4)),
         ],

time: 64.4 us -> 60.7 us (0.943)
  Pallas kernels: 62.6 us -> 58.9 us
    pallas_call x1, Pallas kernels: 62.6 us -> 58.9 us  [dense_shards(): pl.pallas_call(functools.partial(layer_kernel, (tok, width, n_z, cuts)),...]
where the time goes in v4:
time: 60.7 us; the launch traced here: 60.6 us
  Pallas kernels  58.9 us (97%)
  local copies, waits for them, and re-layouts  1.62 us (3%)
    pallas_call x1, Pallas kernels, dense_shards(): pl.pallas_call(functools.partial(layer_kernel, (tok, width, n_z, cuts)),...  58.9 us
    unnamed x1, local copies, waits for them, and re-layouts  1.62 us

profile of v4, /device:TPU:0, one launch (start us, length us, event | category | flops | bytes accessed | tf_op | source)
XLA Modules:
  0.0 60.6 jit_solution(13962925946026140732)
XLA Ops:
  0.0 58.9 %shard_map.100 = bf16[64,1440]{1,0:T(8,128)(2,1)} custom-call(bf16[64,2880]{1,0:T(8,128)(2,1)} %hidden.1, s32[4,64]{1,0:T(4,128)} %bitcast.12, f32[4,64]{1,0:T(4,128)} %bitcast.13, bf16[2880]{0:T(1024)(128)(2,1)} %gain.1, s32[360,2560]{1,0:T(8,128)} %bitcast.8, bf16[90,2560]{1,0:T(8,128)(2,1)} %bitcast.10, bf16[1,2560]{1,0:T(2,128)(2,1)} %gate_bias.1, ...), custom_call_target="tpu_custom_call" | custom-call | tf_op jit(solution)/shard_map/pallas_call | solution.py:742
  58.9 1.6 %copy.12 = bf16[64,1440]{1,0:T(8,128)(2,1)} copy(bf16[64,1440]{1,0:T(8,128)(2,1)} %shard_map.100) | data formatting | bytes 368640

commit v5 on v4

--- a/solution.py
+++ b/solution.py
@@ -548,18 +548,19 @@
 
     parts = range(len(cuts))
 
-    def multiply(b, h, weight):
+    def multiply(b, h, weight, which_parts=parts):
         which = 1 - x if h == 0 else x
-        value = matmul(activated[b], down_weight[which], (1, 1))
+        low, high = cuts[which_parts[0]][0], sum(cuts[which_parts[-1]])
+        value = matmul(activated[b], down_weight[which, low:high, :], (1, 1))
         if h == 1:
-            value = value + bias_part[...]
+            value = value + bias_part[:, low:high]
         value = value * weight
         for i in range(2):
             first = value[2 * i * tok : (2 * i + 1) * tok]
             second = value[(2 * i + 1) * tok : (2 * i + 2) * tok]
-            pair_out[b, h, i] = jnp.where(core == 0, second, first).astype(BF16)
-            kept[b, h, i] = jnp.where(core == 0, first, second).astype(BF16)
-        for q in parts:
+            pair_out[b, h, i, :, low:high] = jnp.where(core == 0, second, first).astype(BF16)
+            kept[b, h, i, :, low:high] = jnp.where(core == 0, first, second).astype(BF16)
+        for q in which_parts:
             pair_copy(b, h, q).start()
 
     def fold_pair(b, h, q):
@@ -623,7 +624,9 @@
     near_weight = weights_of(0)
     mixed = 512
     tiles = gate_cols // mixed
-    steps = decode_steps(1 - x, middle_step, pair_steps) + decode_steps(x, own_ahead, pair_steps)
+    own_steps = decode_steps(x, own_ahead, pair_steps)
+    early = len(own_steps) // 2
+    steps = decode_steps(1 - x, middle_step, pair_steps) + own_steps[:early]
     services = {
         0: [lambda: later_arrives(3, 1)],
         1: [lambda: arrive_crossed(far, 1, 0), lambda: arrive_crossed(far, 1, 1)],
@@ -640,9 +643,9 @@
         complete(0, s)
         complete(1, s)
     far_weight = weights_of(1)
-    gate_tile(1, 0, gate_cols, [])
-    multiply(1, 0, far_weight)
-    multiply(1, 1, far_weight)
+    gate_tile(1, 0, gate_cols, own_steps[early:])
+    multiply(1, 0, far_weight, parts[:2])
+    multiply(1, 0, far_weight, parts[2:])
 
     def send(b, which, q):
         for i in which:
@@ -653,24 +656,26 @@
             side_copy(b, i, q).wait_send()
 
     theirs, ours = (1 - place_in,), (place_in,)
-    for q in parts:
+    for q in parts[:2]:
         fold_pair(1, 0, q)
-        if q < 2:
-            send(1, (0, 1), q)
+        send(1, (0, 1), q)
+    multiply(1, 1, far_weight)
+    for q in parts[2:]:
+        fold_pair(1, 0, q)
     multiply(0, 0, near_weight)
-    multiply(0, 1, near_weight)
     sent(1, (0, 1), 0)
     send(1, (0, 1), 2)
     for q in parts:
         fold_pair(1, 1, q)
+    fold_side(1, 0)
+    multiply(0, 1, near_weight)
+    sent(1, (0, 1), 1)
+    send(1, (0, 1), 3)
     for q in parts:
         fold_pair(0, 0, q)
+    fold_side(1, 1)
     for q in parts:
         fold_pair(0, 1, q)
-    fold_side(1, 0)
-    sent(1, (0, 1), 1)
-    send(1, (0, 1), 3)
-    fold_side(1, 1)
     sent(1, (0, 1), 2)
     send(0, theirs, 0)
     send(0, theirs, 1)

time: 60.7 us -> 59.8 us (0.985)
  Pallas kernels: 58.9 us -> 58.1 us
    pallas_call x1, Pallas kernels: 58.9 us -> 58.1 us  [dense_shards(): pl.pallas_call(functools.partial(layer_kernel, (tok, width, n_z, cuts)),...]
where the time goes in v5:
time: 59.8 us; the launch traced here: 59.7 us
  Pallas kernels  58.1 us (97%)
  local copies, waits for them, and re-layouts  1.62 us (3%)
    pallas_call x1, Pallas kernels, dense_shards(): pl.pallas_call(functools.partial(layer_kernel, (tok, width, n_z, cuts)),...  58.1 us
    unnamed x1, local copies, waits for them, and re-layouts  1.62 us

profile of v5, /device:TPU:0, one launch (start us, length us, event | category | flops | bytes accessed | tf_op | source)
XLA Modules:
  0.0 59.7 jit_solution(390456678170549062)
XLA Ops:
  0.0 58.1 %shard_map.100 = bf16[64,1440]{1,0:T(8,128)(2,1)} custom-call(bf16[64,2880]{1,0:T(8,128)(2,1)} %hidden.1, s32[4,64]{1,0:T(4,128)} %bitcast.12, f32[4,64]{1,0:T(4,128)} %bitcast.13, bf16[2880]{0:T(1024)(128)(2,1)} %gain.1, s32[360,2560]{1,0:T(8,128)} %bitcast.8, bf16[90,2560]{1,0:T(8,128)(2,1)} %bitcast.10, bf16[1,2560]{1,0:T(2,128)(2,1)} %gate_bias.1, ...), custom_call_target="tpu_custom_call" | custom-call | tf_op jit(solution)/shard_map/pallas_call | solution.py:747
  58.1 1.6 %copy.12 = bf16[64,1440]{1,0:T(8,128)(2,1)} copy(bf16[64,1440]{1,0:T(8,128)(2,1)} %shard_map.100) | data formatting | bytes 368640

commit v6 on v5

--- a/solution.py
+++ b/solution.py
@@ -633,17 +633,19 @@
         2: [lambda: crossed(2, 0)],
         3: [lambda: crossed(2, 1), lambda: crossed(3, 0), lambda: crossed(3, 1)],
     }
-    for t in range(tiles):
-        cut = len(steps) * t // tiles, len(steps) * (t + 1) // tiles
+    for t in range(tiles - 1):
+        cut = len(steps) * t // (tiles - 1), len(steps) * (t + 1) // (tiles - 1)
         gate_tile(0, t, mixed, steps[cut[0] : cut[1]])
         for service in services.get(t, []):
             service()
+    for step in own_steps[early:]:
+        step()
     complete(far, 1)
     for s in range(2, n_z):
         complete(0, s)
         complete(1, s)
     far_weight = weights_of(1)
-    gate_tile(1, 0, gate_cols, own_steps[early:])
+    gate_tile(1, 0, gate_cols, [])
     multiply(1, 0, far_weight, parts[:2])
     multiply(1, 0, far_weight, parts[2:])
 
@@ -662,12 +664,13 @@
     multiply(1, 1, far_weight)
     for q in parts[2:]:
         fold_pair(1, 0, q)
-    multiply(0, 0, near_weight)
+    gate_tile(0, tiles - 1, mixed, [])
     sent(1, (0, 1), 0)
     send(1, (0, 1), 2)
     for q in parts:
         fold_pair(1, 1, q)
     fold_side(1, 0)
+    multiply(0, 0, near_weight)
     multiply(0, 1, near_weight)
     sent(1, (0, 1), 1)
     send(1, (0, 1), 3)

time: 59.8 us -> 59.6 us (level)
  no operation moved by 1% of the time
where the time goes in v6:
time: 59.6 us; the launch traced here: 59.5 us
  Pallas kernels  57.9 us (97%)
  local copies, waits for them, and re-layouts  1.62 us (3%)
    pallas_call x1, Pallas kernels, dense_shards(): pl.pallas_call(functools.partial(layer_kernel, (tok, width, n_z, cuts)),...  57.9 us
    unnamed x1, local copies, waits for them, and re-layouts  1.62 us

profile of v6, /device:TPU:0, one launch (start us, length us, event | category | flops | bytes accessed | tf_op | source)
XLA Modules:
  0.0 59.5 jit_solution(3098027097671250267)
XLA Ops:
  0.0 57.9 %shard_map.100 = bf16[64,1440]{1,0:T(8,128)(2,1)} custom-call(bf16[64,2880]{1,0:T(8,128)(2,1)} %hidden.1, s32[4,64]{1,0:T(4,128)} %bitcast.12, f32[4,64]{1,0:T(4,128)} %bitcast.13, bf16[2880]{0:T(1024)(128)(2,1)} %gain.1, s32[360,2560]{1,0:T(8,128)} %bitcast.8, bf16[90,2560]{1,0:T(8,128)(2,1)} %bitcast.10, bf16[1,2560]{1,0:T(2,128)(2,1)} %gate_bias.1, ...), custom_call_target="tpu_custom_call" | custom-call | tf_op jit(solution)/shard_map/pallas_call | solution.py:750
  57.9 1.6 %copy.12 = bf16[64,1440]{1,0:T(8,128)(2,1)} copy(bf16[64,1440]{1,0:T(8,128)(2,1)} %shard_map.100) | data formatting | bytes 368640
